TPU v7x, 32 devices: a whole 2x2x4 slice. The times are simulated.
32 devices in a mesh: ha: 8 (over z, core), wa: 2 (over y), ba: 2 (over x).
Axes of the slice: x: 2, y: 2, z: 4, core: 2. Of those that a mesh axis runs over, the one named last changes fastest.
Arguments:
- tokens: bfloat16 [2, 128, 64, 384], P('ba', 'ha', 'wa'), may hold values from -6 to 6
- cotangent: bfloat16 [2, 128, 64, 384], P('ba', 'ha', 'wa'), may hold values from -6 to 6
- w_qkv: bfloat16 [384, 1152], replicated, may hold values from -0.20412415 to 0.20412415
- w_proj: bfloat16 [384, 384], replicated, may hold values from -0.3125 to 0.3125
- table_logits: float32 [12, 225], replicated, may hold values from -6 to 6
- logit_scale: float32 [12], replicated, may hold values from 1 to 5.5
- gain: float32 [384], replicated, may hold values from 0.5 to 1.5
Outputs:
- d_tokens: bfloat16 [2, 128, 64, 384], P('ba', 'ha', 'wa')
- d_wqkv: float32 [384, 1152], P(None, 'ba')
- d_wproj: float32 [384, 384], P(None, 'ba')
- d_table: float32 [12, 225], replicated
- d_scale: float32 [12], replicated
- d_gain: float32 [384], replicated
All inputs are finite; a program needn't handle non-finite values.
Results may differ from a plain program's by a relative error of at most 0.01.
The roundings to bfloat16 on the way count: a program that leaves them out, or rounds other values in their place, can miss the bound.
Values may be sent and summed in bfloat16 or wider, within the bound.
A program may use at most 64 MiB of HBM per device.

v0:
```python
import math

import jax
import jax.numpy as jnp
from jax import lax
from jax.sharding import PartitionSpec as P

WIN = 8


EPS_NORM = 1e-05
MASK_FILL = -100.0
SCALE_CAP = math.log(100.0)
BIAS_RANGE = 16.0
HIGHEST = lax.Precision.HIGHEST


def from_behind(block, axis, distance):
    devices = range(lax.axis_size(axis))
    route = [((i - distance) % len(devices), i) for i in devices]
    return lax.ppermute(block, axis, route)


def coarse_product(form, left, right):
    return jnp.einsum(form, left, right, preferred_element_type=jnp.float32)


def fine_product(form, left, right):
    return jnp.einsum(form, left, right, precision=HIGHEST)


def to_windows(block, window):
    images, height, width, depth = block.shape
    tiles = block.reshape(images, height // window, window, width // window, window, depth)
    tiles = tiles.transpose(0, 1, 3, 2, 4, 5)
    return tiles.reshape(images, height // window * (width // window), window * window, depth)


def from_windows(tiles, images, height, width, window):
    depth = tiles.shape[-1]
    grid = tiles.reshape(images, height // window, width // window, window, window, depth)
    return grid.transpose(0, 1, 3, 2, 4, 5).reshape(images, height, width, depth)


def position_onehot(window):
    places = jnp.arange(window * window, dtype=jnp.int32)
    row_of = places // window
    col_of = places % window
    offset = (row_of[:, None] - row_of[None, :] + window - 1) * (2 * window - 1) + (
        col_of[:, None] - col_of[None, :] + window - 1
    )
    entries = jnp.arange((2 * window - 1) ** 2, dtype=jnp.int32)
    return (offset.reshape(-1)[:, None] == entries[None, :]).astype(jnp.float32)


def region_of(coords, extent, window):
    return (coords >= extent - window).astype(jnp.int32) + (coords >= extent - window // 2).astype(
        jnp.int32
    )


def region_mask(row_start, col_start, rows, cols, height, width, window):
    row_label = region_of(row_start + jnp.arange(rows, dtype=jnp.int32), height, window)
    col_label = region_of(col_start + jnp.arange(cols, dtype=jnp.int32), width, window)
    labels = row_label[:, None] * 3 + col_label[None, :]
    labels = labels.reshape(rows // window, window, cols // window, window).transpose(0, 2, 1, 3)
    labels = labels.reshape(-1, window * window)
    return jnp.where(labels[:, :, None] != labels[:, None, :], MASK_FILL, 0.0).astype(jnp.float32)


def grads_region(block, grad_block, row_start, col_start, height, width, window, params):
    w_qkv, w_proj, table_logits, logit_scale, gain = params
    images, rows, cols, depth = block.shape
    heads = logit_scale.shape[0]
    head_dim = depth // heads
    tiles = to_windows(block, window)
    grad_tiles = to_windows(grad_block, window)
    count = tiles.shape[1]
    length = window * window
    flat = tiles.reshape(-1, depth)
    qkv = jnp.dot(flat, w_qkv, preferred_element_type=jnp.float32).astype(jnp.bfloat16)
    qkv = qkv.reshape(images, count, length, 3, heads, head_dim)
    query = qkv[:, :, :, 0].astype(jnp.float32)
    keys = qkv[:, :, :, 1].astype(jnp.float32)
    values = qkv[:, :, :, 2]
    query_inv = lax.rsqrt(jnp.sum(query * query, -1, keepdims=True) + 1.0)
    key_inv = lax.rsqrt(jnp.sum(keys * keys, -1, keepdims=True) + 1.0)
    unit_query = query * query_inv
    unit_key = keys * key_inv
    scale = jnp.exp(jnp.minimum(logit_scale, SCALE_CAP))
    onehot = position_onehot(window)
    sigma = jax.nn.sigmoid(table_logits)
    rel_bias = jnp.dot(sigma * BIAS_RANGE, onehot.T, precision=HIGHEST).reshape(
        heads, length, length
    )
    mask = region_mask(row_start, col_start, rows, cols, height, width, window)
    cosine = fine_product("bnqhd,bnkhd->bnhqk", unit_query, unit_key)
    scores = scale[:, None, None] * cosine + rel_bias[None, None] + mask[None, :, None]
    top = jnp.max(scores, -1, keepdims=True)
    expo = jnp.exp(scores - top)
    probs = expo / jnp.sum(expo, -1, keepdims=True)
    probs_low = probs.astype(jnp.bfloat16)
    attended = (
        coarse_product("bnhqk,bnkhd->bnqhd", probs_low, values)
        .astype(jnp.bfloat16)
        .reshape(-1, depth)
    )
    proj = jnp.dot(attended, w_proj, preferred_element_type=jnp.float32)
    centre = proj - jnp.mean(proj, -1, keepdims=True)
    inv_std = lax.rsqrt(jnp.mean(centre * centre, -1, keepdims=True) + EPS_NORM)
    normed = centre * inv_std
    upstream = grad_tiles.reshape(-1, depth).astype(jnp.float32)
    d_gain = jnp.sum(upstream * normed, 0)
    scaled = upstream * gain
    d_proj = inv_std * (
        scaled
        - jnp.mean(scaled, -1, keepdims=True)
        - normed * jnp.mean(scaled * normed, -1, keepdims=True)
    )
    d_proj = d_proj.astype(jnp.bfloat16)
    d_wproj = jnp.dot(attended.T, d_proj, preferred_element_type=jnp.float32)
    d_att = jnp.dot(d_proj, w_proj.T, preferred_element_type=jnp.float32).astype(jnp.bfloat16)
    d_att = d_att.reshape(images, count, length, heads, head_dim)
    d_probs = coarse_product("bnqhd,bnkhd->bnhqk", d_att, values)
    d_values = coarse_product("bnhqk,bnqhd->bnkhd", probs_low, d_att)
    d_scores = probs * (d_probs - jnp.sum(d_probs * probs, -1, keepdims=True))
    d_bias = jnp.sum(d_scores, (0, 1)).reshape(heads, length * length)
    d_table = jnp.dot(d_bias, onehot, precision=HIGHEST) * (BIAS_RANGE * sigma * (1.0 - sigma))
    live = (logit_scale < SCALE_CAP).astype(jnp.float32)
    d_scale = jnp.sum(d_scores * cosine, (0, 1, 3, 4)) * scale * live
    d_cos = d_scores * scale[:, None, None]
    d_unit_q = fine_product("bnhqk,bnkhd->bnqhd", d_cos, unit_key)
    d_unit_k = fine_product("bnhqk,bnqhd->bnkhd", d_cos, unit_query)
    d_query = query_inv * (
        d_unit_q - unit_query * jnp.sum(unit_query * d_unit_q, -1, keepdims=True)
    )
    d_key = key_inv * (d_unit_k - unit_key * jnp.sum(unit_key * d_unit_k, -1, keepdims=True))
    d_qkv = jnp.stack([d_query, d_key, d_values], 3).astype(jnp.bfloat16).reshape(-1, 3 * depth)
    d_wqkv = jnp.dot(flat.T, d_qkv, preferred_element_type=jnp.float32)
    d_flat = jnp.dot(d_qkv, w_qkv.T, preferred_element_type=jnp.float32).astype(jnp.bfloat16)
    d_block = from_windows(d_flat.reshape(images, count, length, depth), images, rows, cols, window)
    return (d_block, (d_wqkv, d_wproj, d_table, d_scale, d_gain))


def shift_in(tokens, cotangent, shift):
    stacked = jnp.stack([tokens, cotangent])
    below = from_behind(stacked[:, :, :shift], "ha", -1)
    tall = jnp.concatenate([stacked[:, :, shift:], below], 2)
    beside = from_behind(tall[:, :, :, :shift], "wa", -1)
    moved = jnp.concatenate([tall[:, :, :, shift:], beside], 3)
    return (moved[0], moved[1])


def shift_out(grads, shift):
    rows = grads.shape[1]
    cols = grads.shape[2]
    right = from_behind(grads[:, :, cols - shift :], "wa", 1)
    wide = jnp.concatenate([right, grads[:, :, : cols - shift]], 2)
    lower = from_behind(wide[:, rows - shift :], "ha", 1)
    return jnp.concatenate([lower, wide[:, : rows - shift]], 1)


def shards(tokens, cotangent, w_qkv, w_proj, table_logits, logit_scale, gain):
    rows = tokens.shape[1]
    cols = tokens.shape[2]
    shift = WIN // 2
    height = rows * lax.axis_size("ha")
    width = cols * lax.axis_size("wa")
    row_base = lax.axis_index("ha") * rows
    col_base = lax.axis_index("wa") * cols
    params = (w_qkv, w_proj, table_logits, logit_scale, gain)
    moved, moved_grad = shift_in(tokens, cotangent, shift)
    d_moved, parts = grads_region(moved, moved_grad, row_base, col_base, height, width, WIN, params)
    back = shift_out(d_moved, shift)
    d_tokens = (cotangent.astype(jnp.float32) + back.astype(jnp.float32)).astype(jnp.bfloat16)
    d_wqkv, d_wproj, d_table, d_scale, d_gain = parts
    half_qkv, half_proj = (
        lax.psum_scatter(d_wqkv.astype(jnp.bfloat16), "ba", scatter_dimension=1, tiled=True).astype(
            jnp.float32
        ),
        lax.psum_scatter(
            d_wproj.astype(jnp.bfloat16), "ba", scatter_dimension=1, tiled=True
        ).astype(jnp.float32),
    )
    half_qkv, half_proj = lax.psum((half_qkv, half_proj), ("ha", "wa"))
    d_table, d_scale, d_gain = lax.psum((d_table, d_scale, d_gain), ("ha", "wa", "ba"))
    return (d_tokens, half_qkv, half_proj, d_table, d_scale, d_gain)


def solution(mesh):
    return jax.shard_map(
        shards,
        mesh=mesh,
        in_specs=(P("ba", "ha", "wa", None), P("ba", "ha", "wa", None), P(), P(), P(), P(), P()),
        out_specs=(P("ba", "ha", "wa", None), P(None, "ba"), P(None, "ba"), P(), P(), P()),
        check_vma=False,
    )
```

profile of v0, /device:TPU:0, one launch (start us, length us, event | category | flops | bytes accessed | tf_op | source)
XLA Modules:
  0.0 213.7 jit_solution(15621993046436900654)
XLA Ops:
  8.3 4.6 %collective-permute-start = (bf16[2,1,4,32,384]{4,3,2,1,0:T(8,128)(2,1)S(1)}, bf16[2,1,4,32,384]{4,3,2,1,0:T(8,128)(2,1)S(1)}, u32[]{:S(2)}, u32[]{:S(2)}) collective-permute-start(bf16[2,1,4,32,384]{4,3,2,1,0:T(8,128)(2,1)S(1)} %pad_maximum_fusion.2), channel_id=1, source_target_pairs={{4,0},{8,4},{12,8},{16,12},{20,16},{24,20},{28,24},{0,28},{5,1},{9... | collective-permute-start | bytes 589832 | tf_op jit(solution)/shard_map/ppermute | solution.py:21
  15.2 2.0 fusion.2
  18.3 1.6 collective-permute-start.1
  20.2 2.8 %collective-permute-done.1 = bf16[2,1,16,4,384]{4,3,2,1,0:T(4,128)(2,1)S(1)} collective-permute-done((bf16[2,1,16,4,384]{4,3,2,1,0:T(4,128)(2,1)S(1)}, bf16[2,1,16,4,384]{4,3,2,1,0:T(4,128)(2,1)S(1)}, u32[]{:S(2)}, u32[]{:S(2)}) %collective-permute-start.1) | collective-permute-done | bytes 98336 | tf_op jit(solution)/shard_map/ppermute | solution.py:21
  26.1 2.7 %reshape.449 = bf16[1,8,64,3,12,32]{2,1,5,4,3,0:T(8,128)(2,1)} reshape(bf16[512,1152]{0,1:T(8,128)(2,1)S(1)} %copy.82) | data formatting | bytes 2359296 | tf_op jit(solution)/shard_map/reshape | solution.py:82
  28.9 1.8 fusion.67
  31.4 5.2 %fusion.29 = f32[8,12,64,64]{2,3,1,0:T(8,128)S(1)} fusion(f32[8,64,12]{1,2,0:T(8,128)S(1)} %add_rsqrt_fusion.1, f32[8,64,12]{1,2,0:T(8,128)S(1)} %add_rsqrt_fusion, bf16[1,8,64,1,12,32]{2,1,5,4,3,0:T(8,128)(2,1)S(1)} %get-tuple-element.16, bf16[1,8,64,1,12,32]{2,1,5,4,3,0:T(8,128)(2,1)S(1)} %get-tuple-element.17), kind=kOutput, calls=%fused_computation.41 | convolution fusion | flops 151781376 | bytes 2408448 | tf_op jit(solution)/shard_map/bnqhd,bnkhd->bnhqk/dot_general | solution.py:29
  41.8 1.5 fusion.69
  44.5 2.3 %copy.90 = f32[512,384]{0,1:T(8,128)} copy(f32[512,384]{1,0:T(8,128)} %bitcast.140) | data formatting | bytes 1572864 | tf_op jit(solution)/shard_map/convert_element_type | solution.py:112
  47.9 1.4 multiply_reduce_fusion.2
  49.5 1.4 multiply_convert_fusion
  52.7 1.3 reshape.452
  54.0 3.7 %multiply_reduce_fusion.1 = (f32[8,12,64]{2,1,0:T(8,128)S(1)}, f32[8,12,64,64]{2,3,1,0:T(8,128)S(1)}) fusion(f32[8,12,64,64]{2,3,1,0:T(8,128)} %copy-done.3, f32[8,12,64]{2,1,0:T(8,128)S(1)} %get-tuple-element.21, bf16[1,8,64,1,12,32]{2,1,5,4,3,0:T(8,128)(2,1)} %copy-done.14, bf16[8,64,12,32]{1,0,3,2:T(8,128)(2,1)} %reshape.452), kind=kOutput, calls=%fused_computation.7 | convolution fusion | flops 26339328 | bytes 3981312 | tf_op jit(solution)/shard_map/bnqhd,bnkhd->bnhqk/dot_general | solution.py:25
  58.3 2.2 %multiply_reduce_fusion = (f32[12]{0:T(128)S(1)}, f32[12,64,64]{1,2,0:T(8,128)}, f32[8,12,64,64]{2,3,1,0:T(8,128)S(1)}) fusion(f32[8,12,64,64]{2,3,1,0:T(8,128)S(1)} %copy-done.2, f32[8,12,64,64]{2,3,1,0:T(8,128)S(1)} %get-tuple-element.26, f32[8,12,64]{2,1,0:T(8,128)S(1)} %get-tuple-element.25, f32[8,12,64,64]{2,3,1,0:T(8,128)S(1)} %copy-done.4, ...), kind=kLoop, calls=%fused_computation.5 | loop fusion | flops 2310132 | bytes 6537264 | tf_op jit(solution)/shard_map/reduce_sum | solution.py:130
  60.4 4.3 %fusion.22 = (f32[8,64,12]{1,2,0:T(8,128)S(1)}, f32[8,12,32,64]{3,2,1,0:T(8,128)}) fusion(f32[8,64,12]{1,2,0:T(8,128)S(1)} %add_rsqrt_fusion.1, bf16[1,8,64,1,12,32]{2,1,5,4,3,0:T(8,128)(2,1)S(1)} %get-tuple-element.17, f32[8,12,64,64]{2,3,1,0:T(8,128)S(1)} %get-tuple-element.15, f32[12]{0:T(128)S(1)} %minimum_exponential_fusion, ...), kind=kOutput, calls=%fused_computation.35 | convolution fusion | flops 152561664 | bytes 3219504 | tf_op jit(solution)/shard_map/bnhqk,bnkhd->bnqhd/dot_general | solution.py:29
  64.7 6.8 %fusion.18 = (f32[8,64,12]{1,2,0:T(8,128)}, f32[8,12,32,64]{3,2,1,0:T(8,128)}) fusion(f32[8,64,12]{1,2,0:T(8,128)S(1)} %add_rsqrt_fusion, bf16[1,8,64,1,12,32]{2,1,5,4,3,0:T(8,128)(2,1)S(1)} %get-tuple-element.16, f32[8,12,64,64]{2,3,1,0:T(8,128)S(1)} %get-tuple-element.15, f32[12]{0:T(128)S(1)} %minimum_exponential_fusion, ...), kind=kOutput, calls=%fused_computation.31 | convolution fusion | flops 152561664 | bytes 3219504 | tf_op jit(solution)/shard_map/bnhqk,bnqhd->bnkhd/dot_general | solution.py:29
  72.8 2.6 %fusion.21 = (bf16[1,8,64,1,12,32]{2,5,4,1,3,0:T(8,128)(2,1)S(1)}, bf16[1,8,64,1,12,32]{2,5,4,1,3,0:T(8,128)(2,1)S(1)}) fusion(f32[8,12,32,64]{3,2,1,0:T(8,128)} %get-tuple-element.28, f32[8,64,12]{1,2,0:T(8,128)} %get-tuple-element.27, f32[8,64,12]{1,2,0:T(8,128)S(1)} %add_rsqrt_fusion, bf16[1,8,64,1,12,32]{2,1,5,4,3,0:T(8,128)(2,1)S(1)} %get-tuple-element.16, ...), kind=kLoop, calls=%fused_computation.34 | loop fusion | flops 2359296 | bytes 3244032 | tf_op jit(solution)/shard_map/stack | solution.py:138
  76.1 2.7 %copy.98 = bf16[1,8,64,3,12,32]{2,1,5,4,3,0:T(8,128)(2,1)S(1)} copy(bf16[1,8,64,3,12,32]{2,5,4,1,3,0:T(8,128)(2,1)S(1)} %maximum_convert_fusion) | data formatting | bytes 2359296 | tf_op jit(solution)/shard_map/convert_element_type | solution.py:138
  78.8 2.4 %convert_element_type.207 = bf16[512,1152]{0,1:T(8,128)(2,1)} reshape(bf16[1,8,64,3,12,32]{2,1,5,4,3,0:T(8,128)(2,1)S(1)} %copy.98) | data formatting | bytes 2359296 | tf_op jit(solution)/shard_map/convert_element_type | solution.py:138
  81.2 3.1 %convolution_convert_fusion.1 = bf16[384,1152]{0,1:T(8,128)(2,1)} fusion(bf16[512,1152]{0,1:T(8,128)(2,1)} %convert_element_type.207, bf16[512,384]{1,0:T(8,128)(2,1)} %bitcast.142), kind=kOutput, calls=%fused_computation.15 | convolution fusion | flops 453427200 | bytes 2457600 | tf_op jit(solution)/shard_map/dot_general | solution.py:139
  86.5 1.6 collective-permute-start.2
  88.1 1.4 fusion.41
  90.8 39.5 %all-reduce = (f32[12,225]{1,0:T(8,128)}, f32[12]{0:T(128)}, f32[384]{0:T(512)}) all-reduce(f32[12,225]{1,0:T(8,128)S(1)} %fusion.41, f32[12]{0:T(128)S(1)} %compare_select_fusion.1, f32[384]{0:T(512)S(1)} %get-tuple-element.8), channel_id=1, replica_groups=mesh['ha'=8,'wa'=2,'ba'=2] {'ha','wa','ba'}, use_global_device_ids=true, to_apply=%region_16.17 | all-reduce | flops 3096 | bytes 24768 | tf_op jit(solution)/shard_map/psum | solution.py:186
  131.2 75.2 %all-reduce.3 = (f32[384,576]{0,1:T(8,128)}, f32[384,192]{0,1:T(8,128)}) all-reduce(bf16[384,576]{0,1:T(8,128)(2,1)} %reduce-scatter.3.cloned.1.call-done, bf16[384,192]{0,1:T(8,128)(2,1)} %reduce-scatter.5.cloned.1.call-done), channel_id=1, replica_groups=mesh['ha'=8,'wa'=2,'ba'=2] {'ha','wa'}, use_global_device_ids=true, to_apply=%region_12.13 | all-reduce | flops 294912 | bytes 1769472 | tf_op jit(solution)/shard_map/psum | solution.py:185
  (99 shorter events, 24.6 us)
Async XLA Ops:
  7.2 17.5 %copy-start = (bf16[384,1152]{1,0:T(8,128)(2,1)S(1)}, bf16[384,1152]{1,0:T(8,128)(2,1)}, u32[]{:S(2)}) copy-start(bf16[384,1152]{1,0:T(8,128)(2,1)} %param.9) | copy-start | bytes 2654212
  7.2 8.0 %copy-start.17 = (f32[12,225]{1,0:T(8,128)S(1)}, f32[12,225]{1,0:T(8,128)}, u32[]{:S(2)}) copy-start(f32[12,225]{1,0:T(8,128)} %param.11) | copy-start | bytes 32404
  7.2 124.1 %reduce-scatter.5.cloned.1.call-start = ((), (), s32[]{:S(2)}) async-start(), calls=%async_computation.3 | async-start | bytes 442368 | tf_op jit(solution)/shard_map/reduce_scatter | solution.py:181
  8.3 10.0 %collective-permute-start = (bf16[2,1,4,32,384]{4,3,2,1,0:T(8,128)(2,1)S(1)}, bf16[2,1,4,32,384]{4,3,2,1,0:T(8,128)(2,1)S(1)}, u32[]{:S(2)}, u32[]{:S(2)}) collective-permute-start(bf16[2,1,4,32,384]{4,3,2,1,0:T(8,128)(2,1)S(1)} %pad_maximum_fusion.2), channel_id=1, source_target_pairs={{4,0},{8,4},{12,8},{16,12},{20,16},{24,20},{28,24},{0,28},{5,1},{9... | collective-permute-start | bytes 589832 | tf_op jit(solution)/shard_map/ppermute | solution.py:21
  14.0 4.3 %copy-start.18 = (f32[12]{0:T(128)S(1)}, f32[12]{0:T(128)}, u32[]{:S(2)}) copy-start(f32[12]{0:T(128)} %param.12) | copy-start | bytes 148
  18.3 4.7 %collective-permute-start.1 = (bf16[2,1,16,4,384]{4,3,2,1,0:T(4,128)(2,1)S(1)}, bf16[2,1,16,4,384]{4,3,2,1,0:T(4,128)(2,1)S(1)}, u32[]{:S(2)}, u32[]{:S(2)}) collective-permute-start(bf16[2,1,16,4,384]{4,3,2,1,0:T(4,128)(2,1)S(1)} %pad_maximum_fusion.4), channel_id=1, source_target_pairs={{2,0},{0,2},{3,1},{1,3},{6,4},{4,6},{7,5},{5,7},{10,8},{8,10},{11,... | collective-permute-start | bytes 294920 | tf_op jit(solution)/shard_map/ppermute | solution.py:21
  30.7 7.7 %copy-start.14 = (bf16[1,8,64,1,12,32]{2,1,5,4,3,0:T(8,128)(2,1)}, bf16[1,8,64,1,12,32]{2,1,5,4,3,0:T(8,128)(2,1)S(1)}, u32[]{:S(2)}) copy-start(bf16[1,8,64,1,12,32]{2,1,5,4,3,0:T(8,128)(2,1)S(1)} %get-tuple-element.18) | copy-start | bytes 1179652
  31.4 5.2 %copy-start.10 = (f32[12,64,64]{1,2,0:T(8,128)S(1)}, f32[12,64,64]{1,2,0:T(8,128)}, u32[]{:S(2)}) copy-start(f32[12,64,64]{1,2,0:T(8,128)} %copy.85) | copy-start | bytes 589828
  31.4 5.2 %copy-start.13 = (f32[8,64,64]{1,2,0:T(8,128)S(1)}, f32[8,64,64]{1,2,0:T(8,128)}, u32[]{:S(2)}) copy-start(f32[8,64,64]{1,2,0:T(8,128)} %compare_select_fusion) | copy-start | bytes 393220
  36.6 1.7 copy-start.1
  38.3 1.7 copy-start.3
  41.8 1.7 copy-start.6
  43.6 3.2 %copy-start.16 = (f32[384]{0:T(512)S(1)}, f32[384]{0:T(512)}, u32[]{:S(2)}) copy-start(f32[384]{0:T(512)} %param.13) | copy-start | bytes 4612
  49.5 1.4 copy-start.12
  49.5 1.9 copy-start.5
  54.0 3.7 %copy-start.2 = (f32[8,12,64,64]{2,3,1,0:T(8,128)S(1)}, f32[8,12,64,64]{2,3,1,0:T(8,128)}, u32[]{:S(2)}) copy-start(f32[8,12,64,64]{2,3,1,0:T(8,128)} %copy-done.1) | copy-start | bytes 4718596
  54.0 4.3 %copy-start.4 = (f32[8,12,64,64]{2,3,1,0:T(8,128)S(1)}, f32[8,12,64,64]{2,3,1,0:T(8,128)}, u32[]{:S(2)}) copy-start(f32[8,12,64,64]{2,3,1,0:T(8,128)} %copy-done.3) | copy-start | bytes 4718596
  64.7 6.8 %copy-start.15 = (bf16[8,64,12,32]{1,0,3,2:T(8,128)(2,1)S(1)}, bf16[8,64,12,32]{1,0,3,2:T(8,128)(2,1)}, u32[]{:S(2)}) copy-start(bf16[8,64,12,32]{1,0,3,2:T(8,128)(2,1)} %reshape.452) | copy-start | bytes 1179652
  72.5 58.7 %reduce-scatter.3.cloned.1.call-start = ((), (), s32[]{:S(2)}) async-start(), calls=%async_computation.2 | async-start | bytes 1327104 | tf_op jit(solution)/shard_map/reduce_scatter | solution.py:178
  81.2 3.1 %copy-start.8 = (f32[12,64,64]{1,2,0:T(8,128)S(1)}, f32[12,64,64]{1,2,0:T(8,128)}, u32[]{:S(2)}) copy-start(f32[12,64,64]{1,2,0:T(8,128)} %get-tuple-element.7) | copy-start | bytes 589828
  84.3 1.3 copy-start.11
  86.4 43.9 %copy-start.7 = (bf16[1,16,32,384]{3,2,1,0:T(8,128)(2,1)S(1)}, bf16[1,16,32,384]{3,2,1,0:T(8,128)(2,1)}, u32[]{:S(2)}) copy-start(bf16[1,16,32,384]{3,2,1,0:T(8,128)(2,1)} %param.8) | copy-start | bytes 1179652
  86.5 4.2 %collective-permute-start.2 = (bf16[1,16,4,384]{3,2,1,0:T(4,128)(2,1)S(1)}, bf16[1,16,4,384]{3,2,1,0:T(4,128)(2,1)S(1)}, u32[]{:S(2)}, u32[]{:S(2)}) collective-permute-start(bf16[1,16,4,384]{3,2,1,0:T(4,128)(2,1)S(1)} %slice.61), channel_id=1, source_target_pairs={{2,0},{0,2},{3,1},{1,3},{6,4},{4,6},{7,5},{5,7},{10,8},{8,10},{11,... | collective-permute-start | bytes 147464 | tf_op jit(solution)/shard_map/ppermute | solution.py:21
  90.7 39.6 %collective-permute-start.3 = (bf16[1,4,32,384]{3,2,1,0:T(8,128)(2,1)S(1)}, bf16[1,4,32,384]{3,2,1,0:T(8,128)(2,1)S(1)}, u32[]{:S(2)}, u32[]{:S(2)}) collective-permute-start(bf16[1,4,32,384]{3,2,1,0:T(8,128)(2,1)S(1)} %pad_maximum_fusion.3), channel_id=1, source_target_pairs={{28,0},{0,4},{4,8},{8,12},{12,16},{16,20},{20,24},{24,28},{29,1},{... | collective-permute-start | bytes 294920 | tf_op jit(solution)/shard_map/ppermute | solution.py:21
  (1 other events, 0.7 us)
Sparse Core Ops, SparseCore 0:
  72.7 11.1 reduce-scatter.4
  86.7 19.1 reduce-scatter.2
where the time goes:
time: 218 us; the launch traced here: 214 us
  blocking collectives  115 us (53%)
  matrix products  32.8 us (15%)
  local copies, waits for them, and re-layouts  22.4 us (10%)
  other arithmetic  16.8 us (8%)
  between operations  14.9 us (7%)
  starting transfers between devices  8.14 us (4%)
  waiting for transfers between devices  4.01 us (2%)
    psum x1, blocking collectives, shards(): half_qkv, half_proj = lax.psum((half_qkv, half_proj), ('ha', 'wa'))  75.2 us
    psum x1, blocking collectives, shards(): lax.psum((d_table, d_scale, d_gain), ('ha', 'wa', 'ba'))  39.5 us
    dot_general x3, matrix products, fine_product(): return jnp.einsum(form, left, right, precision=HIGHEST)  16.3 us
    ppermute x4, starting transfers between devices, from_behind(): return lax.ppermute(block, axis, route)  7.81 us
    dot_general x3, matrix products, coarse_product(): return jnp.einsum(form, left, right, preferred_element_type=jnp.float32)  5.15 us
    convert_element_type x2, local copies, waits for them, and re-layouts, grads_region(): jnp.stack([d_query, d_key, d_values], 3).astype(jnp.bfloat16)  5.15 us
  transfers between devices with their start and end apart: 6, of which 2 were waited for; matrix products, arithmetic and copies ran while one was open for 10% of the time, Pallas kernels for 0%

commit v1 on v0

v1 whole, which is shorter than its diff:
```python
import math

import functools

import jax
import jax.numpy as jnp
import numpy as np
from jax import lax
from jax.experimental import pallas as pl
from jax.experimental.pallas import tpu as pltpu
from jax.sharding import PartitionSpec as P

WIN = 8


EPS_NORM = 1e-05
MASK_FILL = -100.0
SCALE_CAP = math.log(100.0)
BIAS_RANGE = 16.0


def from_behind(block, axis, distance):
    devices = range(lax.axis_size(axis))
    route = [((i - distance) % len(devices), i) for i in devices]
    return lax.ppermute(block, axis, route)


def to_windows(block, window):
    images, height, width, depth = block.shape
    tiles = block.reshape(images, height // window, window, width // window, window, depth)
    tiles = tiles.transpose(0, 1, 3, 2, 4, 5)
    return tiles.reshape(images, height // window * (width // window), window * window, depth)


def from_windows(tiles, images, height, width, window):
    depth = tiles.shape[-1]
    grid = tiles.reshape(images, height // window, width // window, window, window, depth)
    return grid.transpose(0, 1, 3, 2, 4, 5).reshape(images, height, width, depth)


def region_of(coords, extent, window):
    return (coords >= extent - window).astype(jnp.int32) + (coords >= extent - window // 2).astype(
        jnp.int32
    )

GROUP = 4
MESH = pl.DeviceIdType.MESH
VMEM = pl.BlockSpec(memory_space=pltpu.VMEM)
NN = (((1,), (0,)), ((), ()))
NT = (((1,), (1,)), ((), ()))
TN = (((0,), (0,)), ((), ()))


def mxu(left, right, dims):
    return lax.dot_general(left, right, dims, preferred_element_type=jnp.float32)


def split(value):
    high = value.astype(jnp.bfloat16)
    return high, (value - high.astype(jnp.float32)).astype(jnp.bfloat16)


def mxu_fine(left, right, dims):
    high, low = split(left)
    return mxu(high, right, dims) + mxu(low, right, dims)


def same_block(rows, cols, row_size, col_size):
    row = lax.broadcasted_iota(jnp.int32, (rows, cols), 0) // row_size
    col = lax.broadcasted_iota(jnp.int32, (rows, cols), 1) // col_size
    return (row == col).astype(jnp.bfloat16)


def spread(value, width, length):
    tall = jnp.concatenate([value] * GROUP, 0)
    return tall * same_block(tall.shape[0], tall.shape[1], length, width)


def gather_heads(value, width, length):
    lane = lax.broadcasted_iota(jnp.int32, (length, value.shape[1]), 1) // width
    total = jnp.where(lane == 0, value[:length], 0.0)
    for head in range(1, GROUP):
        total = jnp.where(lane == head, value[head * length : (head + 1) * length], total)
    return total


def segment_max(value, size):
    lane = lax.broadcasted_iota(jnp.int32, value.shape, 1) // size
    top = jnp.zeros_like(value)
    for head in range(value.shape[1] // size):
        here = jnp.max(jnp.where(lane == head, value, -jnp.inf), -1, keepdims=True)
        top = jnp.where(lane == head, here, top)
    return top


def local_kernel(
    grid_cols, height, width, window,
    flat_ref, grad_ref, w_qkv_ref, w_proj_ref, bias_ref, scale_ref, gain_ref,
    d_flat_ref, d_wqkv_ref, d_wproj_ref, d_bias_ref, d_cos_ref, d_gain_ref,
    qkv_ref, att_ref, d_att_ref, d_qkv_ref, probs_ref, cos_ref,
):
    tokens, depth = flat_ref.shape
    length = window * window
    count = tokens // length
    groups = bias_ref.shape[0]
    lanes = depth // groups
    head_dim = lanes // GROUP
    wide = GROUP * length
    row_base = lax.axis_index("ha") * (count // grid_cols * window)
    col_base = lax.axis_index("wa") * (grid_cols * window)

    qkv_ref[...] = mxu(flat_ref[...], w_qkv_ref[...], NN).astype(jnp.bfloat16)
    lane_ones = same_block(lanes, wide, head_dim, length)
    wide_ones = same_block(wide, wide, length, length)
    lane_lane = same_block(lanes, lanes, head_dim, head_dim)
    row_ones = jnp.ones((8, lanes), jnp.bfloat16)

    def labels(place, first_row, first_col):
        place = place % length
        row = first_row + place // window
        col = first_col + place % window
        return region_of(row, height, window) * 3 + region_of(col, width, window)

    def load(w, g, part):
        return qkv_ref[
            pl.ds(pl.multiple_of(w * length, length), length),
            part * depth + g * lanes : part * depth + (g + 1) * lanes,
        ]

    def key_row_inv(tall):
        high, low = split(jnp.square(tall.astype(jnp.float32)))
        total = mxu(row_ones, high, NT) + mxu(row_ones, low, NT)
        return lax.rsqrt(total[:1] + 1.0)

    def forward(w, carry):
        first_row = row_base + w // grid_cols * window
        first_col = col_base + w % grid_cols * window
        shape = (length, wide)
        mine = labels(lax.broadcasted_iota(jnp.int32, shape, 0), first_row, first_col)
        other = labels(lax.broadcasted_iota(jnp.int32, shape, 1), first_row, first_col)
        mask = jnp.where(mine != other, MASK_FILL, 0.0)
        for g in range(groups):
            query, key, value = load(w, g, 0), load(w, g, 1), load(w, g, 2)
            tall = spread(key, head_dim, length)
            query_inv = lax.rsqrt(
                mxu_fine(jnp.square(query.astype(jnp.float32)), lane_ones, NN) + 1.0
            )
            cosine = mxu(query, tall, NT) * query_inv * key_row_inv(tall)
            scores = scale_ref[g] * cosine + bias_ref[g] + mask
            expo = jnp.exp(scores - segment_max(scores, length))
            probs = expo / mxu_fine(expo, wide_ones, NN)
            attended = mxu(probs.astype(jnp.bfloat16), spread(value, head_dim, length), NN)
            att_ref[
                pl.ds(pl.multiple_of(w * length, length), length), g * lanes : (g + 1) * lanes
            ] = attended.astype(jnp.bfloat16)
            probs_ref[w, g] = probs
            cos_ref[w, g] = cosine
        return carry

    lax.fori_loop(0, count, forward, 0)

    proj = mxu(att_ref[...], w_proj_ref[...], NN)
    centre = proj - jnp.mean(proj, -1, keepdims=True)
    inv_std = lax.rsqrt(jnp.mean(centre * centre, -1, keepdims=True) + EPS_NORM)
    normed = centre * inv_std
    upstream = grad_ref[...].astype(jnp.float32)
    d_gain_ref[...] = jnp.sum(upstream * normed, 0, keepdims=True)
    scaled = upstream * gain_ref[...]
    d_proj = inv_std * (
        scaled
        - jnp.mean(scaled, -1, keepdims=True)
        - normed * jnp.mean(scaled * normed, -1, keepdims=True)
    )
    d_proj = d_proj.astype(jnp.bfloat16)
    d_wproj_ref[...] = mxu(att_ref[...], d_proj, TN)
    d_att_ref[...] = mxu(d_proj, w_proj_ref[...], NT).astype(jnp.bfloat16)
    d_bias_ref[...] = jnp.zeros_like(d_bias_ref)
    d_cos_ref[...] = jnp.zeros_like(d_cos_ref)

    def backward(w, carry):
        rows = pl.ds(pl.multiple_of(w * length, length), length)
        for g in range(groups):
            query, key, value = load(w, g, 0), load(w, g, 1), load(w, g, 2)
            d_att = d_att_ref[rows, g * lanes : (g + 1) * lanes]
            probs = probs_ref[w, g]
            cosine = cos_ref[w, g]
            tall = spread(key, head_dim, length)
            d_probs = mxu(d_att, spread(value, head_dim, length), NT)
            d_value = gather_heads(
                mxu(probs.astype(jnp.bfloat16), d_att, TN), head_dim, length
            )
            d_scores = probs * (d_probs - mxu_fine(d_probs * probs, wide_ones, NN))
            d_bias_ref[g] += d_scores
            d_cos_ref[g] += d_scores * cosine
            scaled_scores = d_scores * scale_ref[g]
            query32, key32 = query.astype(jnp.float32), key.astype(jnp.float32)
            query_sum = mxu_fine(jnp.square(query32), lane_ones, NN)
            query_wide = lax.rsqrt(query_sum + 1.0)
            query_inv = lax.rsqrt(mxu_fine(jnp.square(query32), lane_lane, NN) + 1.0)
            key_inv = lax.rsqrt(mxu_fine(jnp.square(key32), lane_lane, NN) + 1.0)
            d_unit_q = mxu_fine(scaled_scores * key_row_inv(tall), tall, NN)
            d_unit_k = gather_heads(
                mxu_fine(scaled_scores * query_wide, query, TN), head_dim, length
            )
            unit_q, unit_k = query32 * query_inv, key32 * key_inv
            d_query = query_inv * (d_unit_q - unit_q * mxu_fine(unit_q * d_unit_q, lane_lane, NN))
            d_key = key_inv * (d_unit_k - unit_k * mxu_fine(unit_k * d_unit_k, lane_lane, NN))
            for part, grad in enumerate((d_query, d_key, d_value)):
                d_qkv_ref[rows, part * depth + g * lanes : part * depth + (g + 1) * lanes] = (
                    grad.astype(jnp.bfloat16)
                )
        return carry

    lax.fori_loop(0, count, backward, 0)
    d_wqkv_ref[...] = mxu(flat_ref[...], d_qkv_ref[...], TN)
    d_flat_ref[...] = mxu(d_qkv_ref[...], w_qkv_ref[...], NT).astype(jnp.bfloat16)


def offset_onehot(window):
    places = np.arange(window * window)
    row_of, col_of = places // window, places % window
    offset = (row_of[:, None] - row_of[None, :] + window - 1) * (2 * window - 1) + (
        col_of[:, None] - col_of[None, :] + window - 1
    )
    return jnp.asarray(offset.reshape(-1), jnp.int32)


def three_parts(value):
    high = lax.reduce_precision(value, 8, 7)
    middle = lax.reduce_precision(value - high, 8, 7)
    return jnp.concatenate([high, middle, value - high - middle], 0).astype(jnp.bfloat16)


def local_grads(block, grad_block, row_base, col_base, height, width, window, params):
    w_qkv, w_proj, table_logits, logit_scale, gain = params
    images, rows, cols, depth = block.shape
    heads = logit_scale.shape[0]
    length = window * window
    groups = heads // GROUP
    wide = GROUP * length
    flat = to_windows(block, window).reshape(-1, depth)
    grad_flat = to_windows(grad_block, window).reshape(-1, depth)
    tokens = flat.shape[0]
    count = tokens // length
    scale = jnp.exp(jnp.minimum(logit_scale, SCALE_CAP))
    scale_rows = jnp.repeat(scale.reshape(groups, GROUP), length, 1).reshape(groups, 1, wide)
    sigma = jax.nn.sigmoid(table_logits)
    entries = table_logits.shape[1]
    hot = offset_onehot(window)[None, :] == jnp.arange(entries, dtype=jnp.int32)[:, None]
    hot = hot.astype(jnp.bfloat16)
    parts = jnp.dot(three_parts(sigma * BIAS_RANGE), hot, preferred_element_type=jnp.float32)
    rel_bias = jnp.sum(parts.reshape(3, heads, -1), 0).reshape(groups, GROUP, length, length)
    rel_bias = rel_bias.transpose(0, 2, 1, 3).reshape(groups, length, wide)
    f32, b16 = jnp.float32, jnp.bfloat16
    d_flat, d_wqkv, d_wproj, d_bias, d_cos, d_gain = pl.pallas_call(
        functools.partial(local_kernel, cols // window, height, width, window),
        out_shape=[
            jax.ShapeDtypeStruct((tokens, depth), b16),
            jax.ShapeDtypeStruct((depth, 3 * depth), f32),
            jax.ShapeDtypeStruct((depth, depth), f32),
            jax.ShapeDtypeStruct((groups, length, wide), f32),
            jax.ShapeDtypeStruct((groups, length, wide), f32),
            jax.ShapeDtypeStruct((1, depth), f32),
        ],
        in_specs=[VMEM] * 7,
        out_specs=[VMEM] * 6,
        scratch_shapes=[
            pltpu.VMEM((tokens, 3 * depth), b16),
            pltpu.VMEM((tokens, depth), b16),
            pltpu.VMEM((tokens, depth), b16),
            pltpu.VMEM((tokens, 3 * depth), b16),
            pltpu.VMEM((count, groups, length, wide), f32),
            pltpu.VMEM((count, groups, length, wide), f32),
        ],
        compiler_params=pltpu.CompilerParams(vmem_limit_bytes=48 * 2**20),
        cost_estimate=pl.CostEstimate(
            flops=4_000_000_000, bytes_accessed=8_000_000, transcendentals=400_000
        ),
        name="local_grads",
    )(flat, grad_flat, w_qkv, w_proj, rel_bias, scale_rows, gain.reshape(1, depth))
    heads_bias = d_bias.reshape(groups, length, GROUP, length).transpose(0, 2, 1, 3)
    heads_bias = heads_bias.reshape(heads, length * length)
    sums = lax.dot_general(three_parts(heads_bias), hot, NT, preferred_element_type=jnp.float32)
    d_table = jnp.sum(sums.reshape(3, heads, entries), 0) * (BIAS_RANGE * sigma * (1.0 - sigma))
    live = (logit_scale < SCALE_CAP).astype(jnp.float32)
    d_scale = jnp.sum(d_cos.reshape(groups, length, GROUP, length), (1, 3)).reshape(heads)
    d_scale = d_scale * scale * live
    d_block = from_windows(d_flat.reshape(images, count, length, depth), images, rows, cols, window)
    return (d_block, (d_wqkv, d_wproj, d_table, d_scale, d_gain.reshape(depth)))


def reduce_kernel(
    shape, wqkv_ref, wproj_ref, small_ref, qkv_out, proj_out, small_out,
    core_send, core_get, image_keep, image_send, image_get, near_send, near_get, own, whole, core_all,
    small_core, small_image, small_a, small_b, small_near,
    core_sems, image_sems, near_sems, all_sems, last_sems, tiny_sems,
):
    size_h, size_w = shape
    chips = size_h // 2
    peers = chips * size_w
    ha, wa, ba = lax.axis_index("ha"), lax.axis_index("wa"), lax.axis_index("ba")
    core = ha % 2
    me = wa * chips + ha // 2
    partner = (ha + 1 - 2 * core, wa, ba)
    image = (ha, wa, 1 - ba)

    def peer(step):
        other = lax.rem(me + step, peers)
        return other, (other % chips * 2 + core, other // chips, ba)

    barrier = pltpu.get_barrier_semaphore()
    pl.semaphore_signal(barrier, inc=1, device_id=partner, device_id_type=MESH)
    pl.semaphore_signal(barrier, inc=1, device_id=image, device_id_type=MESH)
    for step in range(1, peers):
        pl.semaphore_signal(barrier, inc=1, device_id=peer(step)[1], device_id_type=MESH)

    depth = wqkv_ref.shape[0]
    half = depth // 2
    q_half, p_half = wqkv_ref.shape[1] // 2, wproj_ref.shape[1] // 2
    f32, b16 = jnp.float32, jnp.bfloat16
    mine = pl.ds(pl.multiple_of(core * half, 16), half)
    theirs = pl.ds(pl.multiple_of((1 - core) * half, 16), half)
    core_send[:, : 2 * q_half] = wqkv_ref[theirs, :].astype(b16)
    core_send[:, 2 * q_half :] = wproj_ref[theirs, :].astype(b16)
    pl.semaphore_wait(barrier, peers + 1)

    def start(src, dst, sems, device):
        copy = pltpu.make_async_remote_copy(
            src_ref=src, dst_ref=dst, send_sem=sems.at[0], recv_sem=sems.at[1],
            device_id=device, device_id_type=MESH,
        )
        copy.start()
        return copy

    big = start(core_send, core_get, core_sems, partner)
    tiny = start(small_ref, small_core, tiny_sems.at[0], partner)
    tiny.wait()
    small_a[...] = small_ref[...] + small_core[...]
    tiny = start(small_a, small_image, tiny_sems.at[1], image)
    big.wait()

    def halves(first):
        q = wqkv_ref[mine, first * q_half : (first + 1) * q_half]
        p = wproj_ref[mine, first * p_half : (first + 1) * p_half]
        gq = core_get[:, first * q_half : (first + 1) * q_half]
        gp = core_get[:, 2 * q_half + first * p_half : 2 * q_half + (first + 1) * p_half]
        return q + gq.astype(f32), p + gp.astype(f32)

    low, high = halves(0), halves(1)
    for part, (a, b) in enumerate(zip(low, high)):
        place = slice(0, q_half) if part == 0 else slice(q_half, q_half + p_half)
        image_send[:, place] = jnp.where(ba == 0, b, a).astype(b16)
        image_keep[:, place] = jnp.where(ba == 0, a, b)
    big = start(image_send, image_get, image_sems, image)
    tiny.wait()
    small_b[...] = small_a[...] + small_image[...]
    tinies = []
    for step in range(1, peers):
        tinies.append(start(small_b, small_near.at[step - 1], tiny_sems.at[step + 1], peer(step)[1]))
    big.wait()
    total = image_keep[...] + image_get[...].astype(f32)
    r, c = near_send.shape[1:]
    split_c = total.shape[1] // c
    for j in range(peers):
        row, col = j // split_c * r, j % split_c * c
        near_send[j] = total[row : row + r, col : col + c].astype(b16)
    copies = []
    for step in range(1, peers):
        other, device = peer(step)
        copies.append(start(near_send.at[other], near_get.at[step - 1], near_sems.at[step - 1], device))
    for copy in tinies:
        copy.wait()
    small = small_b[...]
    for step in range(1, peers):
        small = small + small_near[step - 1]
    small_out[...] = small
    for copy in copies:
        copy.wait()
    total = near_send[me].astype(f32)
    for step in range(1, peers):
        total = total + near_get[step - 1].astype(f32)
    own[...] = total.astype(b16)
    whole[me] = own[...]
    copies = []
    for step in range(1, peers):
        _, device = peer(step)
        copies.append(start(own, whole.at[me], all_sems.at[step - 1], device))
    for copy in copies:
        copy.wait()
    last = start(whole, core_all, last_sems, partner)

    def put(source, first):
        for j in range(peers):
            row, col = j // split_c * r, j % split_c * c
            block = source[j].astype(f32)
            rows = pl.ds(pl.multiple_of(first * half + row, 8), r)
            q_part = max(0, min(c, q_half - col))
            if q_part > 0:
                qkv_out[rows, col : col + q_part] = block[:, :q_part]
            if q_part < c:
                begin = col + q_part - q_half
                proj_out[rows, begin : begin + c - q_part] = block[:, q_part:]

    put(whole, core)
    last.wait()
    put(core_all, 1 - core)


def reduce_all(d_wqkv, d_wproj, small):
    size_h, size_w = lax.axis_size("ha"), lax.axis_size("wa")
    peers = size_h // 2 * size_w
    depth = d_wqkv.shape[0]
    half = depth // 2
    cols = (d_wqkv.shape[1] + d_wproj.shape[1]) // 2
    split_c = 2
    r, c = half * split_c // peers, cols // split_c
    f32, b16 = jnp.float32, jnp.bfloat16
    tiny = small.shape
    return pl.pallas_call(
        functools.partial(reduce_kernel, (size_h, size_w)),
        out_shape=[
            jax.ShapeDtypeStruct((depth, d_wqkv.shape[1] // 2), f32),
            jax.ShapeDtypeStruct((depth, d_wproj.shape[1] // 2), f32),
            jax.ShapeDtypeStruct(tiny, f32),
        ],
        in_specs=[VMEM] * 3,
        out_specs=[VMEM] * 3,
        scratch_shapes=[
            pltpu.VMEM((half, 2 * cols), b16),
            pltpu.VMEM((half, 2 * cols), b16),
            pltpu.VMEM((half, cols), f32),
            pltpu.VMEM((half, cols), b16),
            pltpu.VMEM((half, cols), b16),
            pltpu.VMEM((peers, r, c), b16),
            pltpu.VMEM((peers - 1, r, c), b16),
            pltpu.VMEM((r, c), b16),
            pltpu.VMEM((peers, r, c), b16),
            pltpu.VMEM((peers, r, c), b16),
            pltpu.VMEM(tiny, f32),
            pltpu.VMEM(tiny, f32),
            pltpu.VMEM(tiny, f32),
            pltpu.VMEM(tiny, f32),
            pltpu.VMEM((peers - 1, *tiny), f32),
            pltpu.SemaphoreType.DMA((2,)),
            pltpu.SemaphoreType.DMA((2,)),
            pltpu.SemaphoreType.DMA((peers - 1, 2)),
            pltpu.SemaphoreType.DMA((peers - 1, 2)),
            pltpu.SemaphoreType.DMA((2,)),
            pltpu.SemaphoreType.DMA((peers + 1, 2)),
        ],
        compiler_params=pltpu.CompilerParams(
            collective_id=0, has_side_effects=True, vmem_limit_bytes=48 * 2**20
        ),
        name="reduce_all",
    )(d_wqkv, d_wproj, small)


def can_reduce(d_wqkv):
    peers = lax.axis_size("ha") // 2 * lax.axis_size("wa")
    pairs = lax.axis_size("ha") % 2 == 0 and lax.axis_size("ba") == 2
    return pairs and peers > 1 and d_wqkv.shape[0] % peers == 0 and d_wqkv.shape[0] // peers % 16 == 0


def pack_small(d_table, d_scale, d_gain):
    heads, entries = d_table.shape
    lanes = -(-entries // 128) * 128
    flat = jnp.concatenate([d_scale, d_gain])
    rows = -(-flat.shape[0] // lanes)
    flat = jnp.pad(flat, (0, rows * lanes - flat.shape[0])).reshape(rows, lanes)
    table = jnp.pad(d_table, ((0, 0), (0, lanes - entries)))
    full = jnp.concatenate([table, flat], 0)
    return jnp.pad(full, ((0, -full.shape[0] % 8), (0, 0)))


def unpack_small(full, heads, entries, depth):
    flat = full[heads:].reshape(-1)
    return full[:heads, :entries], flat[:heads], flat[heads : heads + depth]


def shift_in(tokens, cotangent, shift):
    stacked = jnp.stack([tokens, cotangent])
    below = from_behind(stacked[:, :, :shift], "ha", -1)
    tall = jnp.concatenate([stacked[:, :, shift:], below], 2)
    beside = from_behind(tall[:, :, :, :shift], "wa", -1)
    moved = jnp.concatenate([tall[:, :, :, shift:], beside], 3)
    return (moved[0], moved[1])


def shift_out(grads, shift):
    rows = grads.shape[1]
    cols = grads.shape[2]
    right = from_behind(grads[:, :, cols - shift :], "wa", 1)
    wide = jnp.concatenate([right, grads[:, :, : cols - shift]], 2)
    lower = from_behind(wide[:, rows - shift :], "ha", 1)
    return jnp.concatenate([lower, wide[:, : rows - shift]], 1)


def shards(tokens, cotangent, w_qkv, w_proj, table_logits, logit_scale, gain):
    rows = tokens.shape[1]
    cols = tokens.shape[2]
    shift = WIN // 2
    height = rows * lax.axis_size("ha")
    width = cols * lax.axis_size("wa")
    row_base = lax.axis_index("ha") * rows
    col_base = lax.axis_index("wa") * cols
    params = (w_qkv, w_proj, table_logits, logit_scale, gain)
    moved, moved_grad = shift_in(tokens, cotangent, shift)
    d_moved, parts = local_grads(moved, moved_grad, row_base, col_base, height, width, WIN, params)
    back = shift_out(d_moved, shift)
    d_tokens = (cotangent.astype(jnp.float32) + back.astype(jnp.float32)).astype(jnp.bfloat16)
    d_wqkv, d_wproj, d_table, d_scale, d_gain = parts
    if can_reduce(d_wqkv):
        small = pack_small(d_table, d_scale, d_gain)
        half_qkv, half_proj, small = reduce_all(d_wqkv, d_wproj, small)
        d_table, d_scale, d_gain = unpack_small(small, *d_table.shape, d_gain.shape[0])
    else:
        half_qkv, half_proj = (
            lax.psum_scatter(d_wqkv.astype(jnp.bfloat16), "ba", scatter_dimension=1, tiled=True).astype(
                jnp.float32
            ),
            lax.psum_scatter(
                d_wproj.astype(jnp.bfloat16), "ba", scatter_dimension=1, tiled=True
            ).astype(jnp.float32),
        )
        half_qkv, half_proj = lax.psum((half_qkv, half_proj), ("ha", "wa"))
        d_table, d_scale, d_gain = lax.psum((d_table, d_scale, d_gain), ("ha", "wa", "ba"))
    return (d_tokens, half_qkv, half_proj, d_table, d_scale, d_gain)


def solution(mesh):
    return jax.shard_map(
        shards,
        mesh=mesh,
        in_specs=(P("ba", "ha", "wa", None), P("ba", "ha", "wa", None), P(), P(), P(), P(), P()),
        out_specs=(P("ba", "ha", "wa", None), P(None, "ba"), P(None, "ba"), P(), P(), P()),
        check_vma=False,
    )
```

time: 218 us -> 87.9 us (0.40); the launches traced: 214 us -> 87.6 us
  blocking collectives: 115 us -> 0 us
  Pallas kernels: 0 us -> 59.1 us
  matrix products: 32.8 us -> 2.26 us
  local copies, waits for them, and re-layouts: 22.4 us -> 8.47 us
  between operations: 14.9 us -> 0.98 us
  other arithmetic: 16.8 us -> 3.52 us
    psum x2 -> x0, blocking collectives: 115 us -> none  [the longest x1 75.2 us: shards(): half_qkv, half_proj = lax.psum((half_qkv, half_proj), ('ha', 'wa'))]
    pallas_call x0 -> x2, Pallas kernels: none -> 59.1 us  [the longest x1 29.8 us: local_grads(): pl.pallas_call(functools.partial(local_kernel, cols // window, height, wi...]
    dot_general x14 -> x2, matrix products: 32.8 us -> 2.26 us  [the longest x1 1.46 us: local_grads(): jnp.dot(three_parts(sigma * BIAS_RANGE), hot, preferred_element_type=jnp....]
    convert_element_type x7 -> x0, local copies, waits for them, and re-layouts: 9.67 us -> none  [the longest x2 5.15 us: grads_region(): jnp.stack([d_query, d_key, d_values], 3).astype(jnp.bfloat16)]
    reduce_sum x6 -> x4, other arithmetic: 5.54 us -> 0.18 us  [the longest x2 0.12 us: local_grads(): jnp.sum(d_cos.reshape(groups, length, GROUP, length), (1, 3)).reshape(heads)]
  transfers between devices with their start and end apart: 6 -> 4, of which waited for: 2 -> 2; matrix products, arithmetic and copies ran while one was open for 10% -> 11% of each run, Pallas kernels for 0% -> 34%
where the time goes in v1:
time: 87.9 us; the launch traced here: 87.6 us
  Pallas kernels  59.1 us (67%)
  local copies, waits for them, and re-layouts  8.47 us (10%)
  starting transfers between devices  8.16 us (9%)
  waiting for transfers between devices  5.02 us (6%)
  other arithmetic  3.52 us (4%)
  matrix products  2.26 us (3%)
  between operations  0.98 us (1%)
    pallas_call x1, Pallas kernels, local_grads(): pl.pallas_call(functools.partial(local_kernel, cols // window, height, wi...  29.8 us
    pallas_call x1, Pallas kernels, reduce_all(): pl.pallas_call(functools.partial(reduce_kernel, (size_h, size_w)), out_sh...  29.4 us
    ppermute x4, starting transfers between devices, from_behind(): return lax.ppermute(block, axis, route)  8.16 us
    ppermute x4, waiting for transfers between devices, from_behind(): return lax.ppermute(block, axis, route)  5.02 us
    unnamed x33, local copies, waits for them, and re-layouts  3.85 us
  transfers between devices with their start and end apart: 4, of which 2 were waited for; matrix products, arithmetic and copies ran while one was open for 11% of the time, Pallas kernels for 34%

profile of v1, /device:TPU:0, one launch (start us, length us, event | category | flops | bytes accessed | tf_op | source)
XLA Modules:
  0.0 87.6 jit_solution(4728340465275639193)
XLA Ops:
  0.7 1.0 %pad_maximum_fusion.2 = bf16[2,1,4,32,384]{4,3,2,1,0:T(8,128)(2,1)S(1)} fusion(bf16[1,1,16,32,384]{4,3,2,1,0:T(8,128)(2,1)} %bitcast.32, bf16[1,1,16,32,384]{4,3,2,1,0:T(8,128)(2,1)} %bitcast.38), kind=kLoop, calls=%fused_computation.27 | loop fusion | flops 98304 | bytes 983040 | tf_op jit(solution)/shard_map/stack | solution.py:481
  1.6 4.6 %collective-permute-start = (bf16[2,1,4,32,384]{4,3,2,1,0:T(8,128)(2,1)S(1)}, bf16[2,1,4,32,384]{4,3,2,1,0:T(8,128)(2,1)S(1)}, u32[]{:S(2)}, u32[]{:S(2)}) collective-permute-start(bf16[2,1,4,32,384]{4,3,2,1,0:T(8,128)(2,1)S(1)} %pad_maximum_fusion.2), channel_id=1, source_target_pairs={{4,0},{8,4},{12,8},{16,12},{20,16},{24,20},{28,24},{0,28},{5,1},{9... | collective-permute-start | bytes 589832 | tf_op jit(solution)/shard_map/ppermute | solution.py:25
  6.2 0.7 reduce-precision_convert_fusion.3
  6.9 1.5 %fusion.1 = f32[36,4096]{1,0:T(8,128)S(1)} fusion(s32[4096]{0:T(1024)} %constant.13.clone, bf16[12,225]{1,0:T(8,128)(2,1)S(1)} %get-tuple-element.48, bf16[12,225]{1,0:T(8,128)(2,1)S(1)} %get-tuple-element.49, bf16[12,225]{1,0:T(8,128)(2,1)S(1)} %get-tuple-element.47), kind=kOutput, calls=%fused_computation.2 | convolution fusion | flops 67325400 | bytes 622408 | tf_op jit(solution)/shard_map/dot_general | solution.py:251
  9.0 0.3 copy.28
  9.3 0.3 reshape.84.bias_ref
  10.0 1.6 %collective-permute-start.1 = (bf16[2,1,16,4,384]{4,3,2,1,0:T(4,128)(2,1)S(1)}, bf16[2,1,16,4,384]{4,3,2,1,0:T(4,128)(2,1)S(1)}, u32[]{:S(2)}, u32[]{:S(2)}) collective-permute-start(bf16[2,1,16,4,384]{4,3,2,1,0:T(4,128)(2,1)S(1)} %pad_maximum_fusion.4), channel_id=1, source_target_pairs={{2,0},{0,2},{3,1},{1,3},{6,4},{4,6},{7,5},{5,7},{10,8},{8,10},{11,... | collective-permute-start | bytes 294920 | tf_op jit(solution)/shard_map/ppermute | solution.py:25
  11.6 0.2 slice_maximum_fusion
  11.8 2.8 %collective-permute-done.1 = bf16[2,1,16,4,384]{4,3,2,1,0:T(4,128)(2,1)S(1)} collective-permute-done((bf16[2,1,16,4,384]{4,3,2,1,0:T(4,128)(2,1)S(1)}, bf16[2,1,16,4,384]{4,3,2,1,0:T(4,128)(2,1)S(1)}, u32[]{:S(2)}, u32[]{:S(2)}) %collective-permute-start.1) | collective-permute-done | bytes 98336 | tf_op jit(solution)/shard_map/ppermute | solution.py:25
  14.9 29.8 %local_grads.1 = (bf16[512,384]{1,0:T(8,128)(2,1)S(1)}, f32[384,1152]{1,0:T(8,128)S(1)}, f32[384,384]{1,0:T(8,128)S(1)}, f32[3,64,256]{2,1,0:T(8,128)S(1)}, f32[...) custom-call(bf16[512,384]{1,0:T(8,128)(2,1)S(1)} %bitcast.26, bf16[512,384]{1,0:T(8,128)(2,1)S(1)} %bitcast.25, ...), custom_call_target="tpu_custom_call" | custom-call | flops 4000000000 | bytes 8000000 | tf_op jit(solution)/shard_map/local_grads/pallas_call | solution.py:255
  45.3 1.6 %collective-permute-start.2 = (bf16[1,16,4,384]{3,2,1,0:T(4,128)(2,1)S(1)}, bf16[1,16,4,384]{3,2,1,0:T(4,128)(2,1)S(1)}, u32[]{:S(2)}, u32[]{:S(2)}) collective-permute-start(bf16[1,16,4,384]{3,2,1,0:T(4,128)(2,1)S(1)} %slice.62), channel_id=1, source_target_pairs={{2,0},{0,2},{3,1},{1,3},{6,4},{4,6},{7,5},{5,7},{10,8},{8,10},{11,... | collective-permute-start | bytes 147464 | tf_op jit(solution)/shard_map/ppermute | solution.py:25
  47.0 0.8 copy.35
  47.8 1.1 %reshape.89 = f32[12,4096]{1,0:T(8,128)S(1)} reshape(f32[3,4,64,64]{3,2,1,0:T(8,128)} %bitcast.35) | data formatting | bytes 393216 | tf_op jit(solution)/shard_map/reshape | solution.py:282
  49.1 0.8 fusion
  50.0 29.4 %reduce_all.1 = (f32[384,576]{1,0:T(8,128)S(1)}, f32[384,192]{1,0:T(8,128)S(1)}, f32[16,256]{1,0:T(8,128)S(1)}) custom-call(f32[384,1152]{1,0:T(8,128)S(1)} %get-tuple-element.16.wqkv_ref, f32[384,384]{1,0:T(8,128)S(1)} %get-tuple-element.17.wproj_ref, f32[16,256]{1,0:T(8,128)S(1)} %pad.14.small_ref), custom_call_target="tpu_custom_call" | custom-call | tf_op jit(solution)/shard_map/reduce_all/pallas_call | solution.py:419
  79.3 0.7 copy-done
  80.1 0.4 collective-permute-start.3
  80.6 0.5 slice.54
  81.1 0.6 slice.55
  81.7 1.2 %copy.31 = f32[384,576]{0,1:T(8,128)} copy(f32[384,576]{1,0:T(8,128)S(1)} %get-tuple-element.37) | data formatting | bytes 1769472
  83.0 0.9 copy.32
  83.8 2.2 %collective-permute-done.3 = bf16[1,4,32,384]{3,2,1,0:T(8,128)(2,1)S(1)} collective-permute-done((bf16[1,4,32,384]{3,2,1,0:T(8,128)(2,1)S(1)}, bf16[1,4,32,384]{3,2,1,0:T(8,128)(2,1)S(1)}, u32[]{:S(2)}, u32[]{:S(2)}) %collective-permute-start.3) | collective-permute-done | bytes 98336 | tf_op jit(solution)/shard_map/ppermute | solution.py:25
  86.0 0.9 %add_convert_fusion = bf16[1,16,32,384]{3,2,1,0:T(8,128)(2,1)} fusion(bf16[1,16,32,384]{3,2,1,0:T(8,128)(2,1)S(1)} %copy-done.8, bf16[1,16,28,384]{3,2,1,0:T(8,128)(2,1)S(1)} %bitcast.31, bf16[1,16,4,384]{3,2,1,0:T(4,128)(2,1)S(1)} %collective-permute-done.2, bf16[1,4,32,384]{3,2,1,0:T(8,128)(2,1)S(1)} %collective-permute-done.3), kind=kLoop, calls=%fused_computation.10 | loop fusion | flops 1769472 | bytes 1277952 | tf_op jit(solution)/shard_map/convert_element_type | solution.py:510
  87.0 0.6 copy.37
  (62 shorter events, 2.1 us)
Async XLA Ops:
  0.6 7.8 %copy-start.12 = (f32[12]{0:T(128)S(1)}, f32[12]{0:T(128)}, u32[]{:S(2)}) copy-start(f32[12]{0:T(128)} %param.13) | copy-start | bytes 148
  0.6 7.9 %copy-start.11 = (f32[384]{0:T(512)S(1)}, f32[384]{0:T(512)}, u32[]{:S(2)}) copy-start(f32[384]{0:T(512)} %param.14) | copy-start | bytes 4612
  1.6 8.3 %collective-permute-start = (bf16[2,1,4,32,384]{4,3,2,1,0:T(8,128)(2,1)S(1)}, bf16[2,1,4,32,384]{4,3,2,1,0:T(8,128)(2,1)S(1)}, u32[]{:S(2)}, u32[]{:S(2)}) collective-permute-start(bf16[2,1,4,32,384]{4,3,2,1,0:T(8,128)(2,1)S(1)} %pad_maximum_fusion.2), channel_id=1, source_target_pairs={{4,0},{8,4},{12,8},{16,12},{20,16},{24,20},{28,24},{0,28},{5,1},{9... | collective-permute-start | bytes 589832 | tf_op jit(solution)/shard_map/ppermute | solution.py:25
  8.7 1.0 %copy-start.7 = (bf16[1,16,32,384]{3,2,1,0:T(8,128)(2,1)S(1)}, bf16[1,16,32,384]{3,2,1,0:T(8,128)(2,1)}, u32[]{:S(2)}) copy-start(bf16[1,16,32,384]{3,2,1,0:T(8,128)(2,1)} %param.9) | copy-start | bytes 1179652
  8.8 1.1 %copy-start.9 = (bf16[1,16,32,384]{3,2,1,0:T(8,128)(2,1)S(1)}, bf16[1,16,32,384]{3,2,1,0:T(8,128)(2,1)}, u32[]{:S(2)}) copy-start(bf16[1,16,32,384]{3,2,1,0:T(8,128)(2,1)} %param.8) | copy-start | bytes 1179652
  10.0 4.7 %collective-permute-start.1 = (bf16[2,1,16,4,384]{4,3,2,1,0:T(4,128)(2,1)S(1)}, bf16[2,1,16,4,384]{4,3,2,1,0:T(4,128)(2,1)S(1)}, u32[]{:S(2)}, u32[]{:S(2)}) collective-permute-start(bf16[2,1,16,4,384]{4,3,2,1,0:T(4,128)(2,1)S(1)} %pad_maximum_fusion.4), channel_id=1, source_target_pairs={{2,0},{0,2},{3,1},{1,3},{6,4},{4,6},{7,5},{5,7},{10,8},{8,10},{11,... | collective-permute-start | bytes 294920 | tf_op jit(solution)/shard_map/ppermute | solution.py:25
  11.8 3.1 %copy-start.2 = (bf16[384,1152]{1,0:T(8,128)(2,1)S(1)}, bf16[384,1152]{1,0:T(8,128)(2,1)}, u32[]{:S(2)}) copy-start(bf16[384,1152]{1,0:T(8,128)(2,1)} %w_qkv_ref.1) | copy-start | bytes 2654212
  11.8 3.1 %copy-start.3 = (bf16[384,384]{1,0:T(8,128)(2,1)S(1)}, bf16[384,384]{1,0:T(8,128)(2,1)}, u32[]{:S(2)}) copy-start(bf16[384,384]{1,0:T(8,128)(2,1)} %w_proj_ref.1) | copy-start | bytes 884740
  44.7 4.3 %copy-start.13 = (s32[4096]{0:T(1024)S(1)}, s32[4096]{0:T(1024)}, u32[]{:S(2)}) copy-start(s32[4096]{0:T(1024)} %constant.13.clone) | copy-start | bytes 49156
  44.8 5.1 %copy-start.4 = (bf16[1,2,8,4,8,384]{5,4,3,2,1,0:T(8,128)(2,1)}, bf16[1,2,8,4,8,384]{5,4,3,2,1,0:T(8,128)(2,1)S(1)}, u32[]{:S(2)}) copy-start(bf16[1,2,8,4,8,384]{5,4,3,2,1,0:T(8,128)(2,1)S(1)} %copy.29) | copy-start | bytes 1179652
  45.3 34.8 %collective-permute-start.2 = (bf16[1,16,4,384]{3,2,1,0:T(4,128)(2,1)S(1)}, bf16[1,16,4,384]{3,2,1,0:T(4,128)(2,1)S(1)}, u32[]{:S(2)}, u32[]{:S(2)}) collective-permute-start(bf16[1,16,4,384]{3,2,1,0:T(4,128)(2,1)S(1)} %slice.62), channel_id=1, source_target_pairs={{2,0},{0,2},{3,1},{1,3},{6,4},{4,6},{7,5},{5,7},{10,8},{8,10},{11,... | collective-permute-start | bytes 147464 | tf_op jit(solution)/shard_map/ppermute | solution.py:25
  47.8 2.1 %copy-start.10 = (f32[12,225]{1,0:T(8,128)S(1)}, f32[12,225]{1,0:T(8,128)}, u32[]{:S(2)}) copy-start(f32[12,225]{1,0:T(8,128)} %param.12) | copy-start | bytes 32404
  49.9 30.2 %copy-start.5 = (bf16[1,2,8,4,8,384]{5,4,3,2,1,0:T(8,128)(2,1)S(1)}, bf16[1,2,8,4,8,384]{5,4,3,2,1,0:T(8,128)(2,1)}, u32[]{:S(2)}) copy-start(bf16[1,2,8,4,8,384]{5,4,3,2,1,0:T(8,128)(2,1)} %copy-done.4) | copy-start | bytes 1179652
  79.3 0.7 copy-start
  80.1 6.0 %copy-start.6 = (bf16[1,2,8,4,8,384]{5,4,3,2,1,0:T(8,128)(2,1)S(1)}, bf16[1,2,8,4,8,384]{5,4,3,2,1,0:T(8,128)(2,1)}, u32[]{:S(2)}) copy-start(bf16[1,2,8,4,8,384]{5,4,3,2,1,0:T(8,128)(2,1)} %copy-done.4) | copy-start | bytes 1179652
  80.1 6.0 %copy-start.8 = (bf16[1,16,32,384]{3,2,1,0:T(8,128)(2,1)S(1)}, bf16[1,16,32,384]{3,2,1,0:T(8,128)(2,1)}, u32[]{:S(2)}) copy-start(bf16[1,16,32,384]{3,2,1,0:T(8,128)(2,1)} %param.9) | copy-start | bytes 1179652
  80.1 2.9 %copy-start.1 = (f32[384,192]{1,0:T(8,128)S(1)}, f32[384,192]{1,0:T(8,128)}, u32[]{:S(2)}) copy-start(f32[384,192]{1,0:T(8,128)} %copy-done) | copy-start | bytes 884740
  80.1 5.9 %collective-permute-start.3 = (bf16[1,4,32,384]{3,2,1,0:T(8,128)(2,1)S(1)}, bf16[1,4,32,384]{3,2,1,0:T(8,128)(2,1)S(1)}, u32[]{:S(2)}, u32[]{:S(2)}) collective-permute-start(bf16[1,4,32,384]{3,2,1,0:T(8,128)(2,1)S(1)} %pad_maximum_fusion.3), channel_id=1, source_target_pairs={{28,0},{0,4},{4,8},{8,12},{12,16},{16,20},{20,24},{24,28},{29,1},{... | collective-permute-start | bytes 294920 | tf_op jit(solution)/shard_map/ppermute | solution.py:25

commit v2 on v1

--- a/solution.py
+++ b/solution.py
@@ -23,13 +23,6 @@
     devices = range(lax.axis_size(axis))
     route = [((i - distance) % len(devices), i) for i in devices]
     return lax.ppermute(block, axis, route)
-
-
-def to_windows(block, window):
-    images, height, width, depth = block.shape
-    tiles = block.reshape(images, height // window, window, width // window, window, depth)
-    tiles = tiles.transpose(0, 1, 3, 2, 4, 5)
-    return tiles.reshape(images, height // window * (width // window), window * window, depth)
 
 
 def from_windows(tiles, images, height, width, window):
@@ -118,7 +111,7 @@
     def labels(place, first_row, first_col):
         place = place % length
         row = first_row + place // window
-        col = first_col + place % window
+        col = first_col + (place + window // 2) % window
         return region_of(row, height, window) * 3 + region_of(col, width, window)
 
     def load(w, g, part):
@@ -218,7 +211,7 @@
 
 def offset_onehot(window):
     places = np.arange(window * window)
-    row_of, col_of = places // window, places % window
+    row_of, col_of = places // window, (places + window // 2) % window
     offset = (row_of[:, None] - row_of[None, :] + window - 1) * (2 * window - 1) + (
         col_of[:, None] - col_of[None, :] + window - 1
     )
@@ -231,15 +224,13 @@
     return jnp.concatenate([high, middle, value - high - middle], 0).astype(jnp.bfloat16)
 
 
-def local_grads(block, grad_block, row_base, col_base, height, width, window, params):
+def local_grads(flat, grad_flat, cols, height, width, window, params):
     w_qkv, w_proj, table_logits, logit_scale, gain = params
-    images, rows, cols, depth = block.shape
+    depth = flat.shape[1]
     heads = logit_scale.shape[0]
     length = window * window
     groups = heads // GROUP
     wide = GROUP * length
-    flat = to_windows(block, window).reshape(-1, depth)
-    grad_flat = to_windows(grad_block, window).reshape(-1, depth)
     tokens = flat.shape[0]
     count = tokens // length
     scale = jnp.exp(jnp.minimum(logit_scale, SCALE_CAP))
@@ -285,15 +276,95 @@
     live = (logit_scale < SCALE_CAP).astype(jnp.float32)
     d_scale = jnp.sum(d_cos.reshape(groups, length, GROUP, length), (1, 3)).reshape(heads)
     d_scale = d_scale * scale * live
-    d_block = from_windows(d_flat.reshape(images, count, length, depth), images, rows, cols, window)
-    return (d_block, (d_wqkv, d_wproj, d_table, d_scale, d_gain.reshape(depth)))
+    return (d_flat, (d_wqkv, d_wproj, d_table, d_scale, d_gain.reshape(depth)))
+
+
+def shift_in_kernel(
+    size_h, size_w, window, tokens_ref, cot_ref, flat_ref, grad_ref,
+    side_send, row_get, side_get, corner_get, sems,
+):
+    ha, wa, ba = lax.axis_index("ha"), lax.axis_index("wa"), lax.axis_index("ba")
+    up, left = lax.rem(ha + size_h - 1, size_h), lax.rem(wa + size_w - 1, size_w)
+    down, right = lax.rem(ha + 1, size_h), lax.rem(wa + 1, size_w)
+    barrier = pltpu.get_barrier_semaphore()
+    for device in ((down, wa, ba), (ha, right, ba), (down, right, ba)):
+        pl.semaphore_signal(barrier, inc=1, device_id=device, device_id_type=MESH)
+    rows, cols, depth = tokens_ref.shape
+    shift = window // 2
+    tiles = cols // window
+    f32 = jnp.float32
+    for n, ref in enumerate((tokens_ref, cot_ref)):
+        side = ref[:, :window, :].astype(f32).reshape(rows * window, depth)
+        side_send[n] = side.astype(jnp.bfloat16)
+    pl.semaphore_wait(barrier, 3)
+    copies = []
+    for n, ref in enumerate((tokens_ref, cot_ref)):
+        edge = shift * window
+        plan = (
+            (ref.at[pl.ds(0, shift)], row_get.at[n], (up, wa, ba)),
+            (side_send.at[n], side_get.at[n], (ha, left, ba)),
+            (side_send.at[n, pl.ds(0, edge)], corner_get.at[n], (up, left, ba)),
+        )
+        for k, (src, dst, device) in enumerate(plan):
+            copy = pltpu.make_async_remote_copy(
+                src_ref=src, dst_ref=dst, send_sem=sems.at[n, k, 0], recv_sem=sems.at[n, k, 1],
+                device_id=device, device_id_type=MESH,
+            )
+            copy.start()
+            copies.append(copy)
+    for copy in copies:
+        copy.wait()
+    later = lax.broadcasted_iota(jnp.int32, (window, window, depth), 1) >= shift
+    for n, (ref, out) in enumerate(((tokens_ref, flat_ref), (cot_ref, grad_ref))):
+        tall = jnp.concatenate([ref[shift:].astype(f32), row_get[n].astype(f32)], 0)
+        tall = tall.reshape(rows, tiles, window, depth)
+        side = jnp.concatenate(
+            [side_get[n, shift * window :].astype(f32), corner_get[n].astype(f32)], 0
+        ).reshape(rows, window, depth)
+        for down_tile in range(rows // window):
+            span = slice(down_tile * window, (down_tile + 1) * window)
+            for tile in range(tiles):
+                beside = tall[span, tile + 1] if tile + 1 < tiles else side[span]
+                value = jnp.where(later, tall[span, tile], beside)
+                place = (down_tile * tiles + tile) * window * window
+                out[place : place + window * window, :] = value.reshape(
+                    window * window, depth
+                ).astype(jnp.bfloat16)
+
+
+def shift_in(tokens, cotangent, window):
+    _, rows, cols, depth = tokens.shape
+    b16 = jnp.bfloat16
+    shift = window // 2
+    flat = jax.ShapeDtypeStruct((rows * cols, depth), b16)
+    return pl.pallas_call(
+        functools.partial(shift_in_kernel, lax.axis_size("ha"), lax.axis_size("wa"), window),
+        out_shape=[flat, flat],
+        in_specs=[VMEM] * 2,
+        out_specs=[VMEM] * 2,
+        scratch_shapes=[
+            pltpu.VMEM((2, rows * window, depth), b16),
+            pltpu.VMEM((2, shift, cols, depth), b16),
+            pltpu.VMEM((2, rows * window, depth), b16),
+            pltpu.VMEM((2, shift * window, depth), b16),
+            pltpu.SemaphoreType.DMA((2, 3, 2)),
+        ],
+        compiler_params=pltpu.CompilerParams(
+            collective_id=1, has_side_effects=True, vmem_limit_bytes=32 * 2**20
+        ),
+        name="shift_in",
+    )(tokens.reshape(rows, cols, depth), cotangent.reshape(rows, cols, depth))
+
+
+CHUNKS = 3
 
 
 def reduce_kernel(
-    shape, wqkv_ref, wproj_ref, small_ref, qkv_out, proj_out, small_out,
+    shape, window, wqkv_ref, wproj_ref, small_ref, d_flat_ref, cot_ref,
+    qkv_out, proj_out, small_out, tokens_out,
     core_send, core_get, image_keep, image_send, image_get, near_send, near_get, own, whole, core_all,
-    small_core, small_image, small_a, small_b, small_near,
-    core_sems, image_sems, near_sems, all_sems, last_sems, tiny_sems,
+    small_core, small_image, small_a, small_b, small_near, side_get, row_get, corner_get,
+    core_sems, image_sems, near_sems, all_sems, last_sems, tiny_sems, halo_sems,
 ):
     size_h, size_w = shape
     chips = size_h // 2
@@ -303,26 +374,41 @@
     me = wa * chips + ha // 2
     partner = (ha + 1 - 2 * core, wa, ba)
     image = (ha, wa, 1 - ba)
+    up, left = lax.rem(ha + size_h - 1, size_h), lax.rem(wa + size_w - 1, size_w)
+    down, right = lax.rem(ha + 1, size_h), lax.rem(wa + 1, size_w)
 
     def peer(step):
         other = lax.rem(me + step, peers)
         return other, (other % chips * 2 + core, other // chips, ba)
 
     barrier = pltpu.get_barrier_semaphore()
-    pl.semaphore_signal(barrier, inc=1, device_id=partner, device_id_type=MESH)
-    pl.semaphore_signal(barrier, inc=1, device_id=image, device_id_type=MESH)
-    for step in range(1, peers):
-        pl.semaphore_signal(barrier, inc=1, device_id=peer(step)[1], device_id_type=MESH)
+    greeted = [partner, image, (up, wa, ba), (ha, left, ba), (up, left, ba)]
+    greeted += [peer(step)[1] for step in range(1, peers)]
+    for device in greeted:
+        pl.semaphore_signal(barrier, inc=1, device_id=device, device_id_type=MESH)
 
     depth = wqkv_ref.shape[0]
     half = depth // 2
     q_half, p_half = wqkv_ref.shape[1] // 2, wproj_ref.shape[1] // 2
+    span = image_keep.shape[2]
     f32, b16 = jnp.float32, jnp.bfloat16
     mine = pl.ds(pl.multiple_of(core * half, 16), half)
     theirs = pl.ds(pl.multiple_of((1 - core) * half, 16), half)
-    core_send[:, : 2 * q_half] = wqkv_ref[theirs, :].astype(b16)
-    core_send[:, 2 * q_half :] = wproj_ref[theirs, :].astype(b16)
-    pl.semaphore_wait(barrier, peers + 1)
+
+    def piece(rows, side, k):
+        low, high = k * span, (k + 1) * span
+        parts = []
+        if low < q_half:
+            parts.append(wqkv_ref[rows, side * q_half + low : side * q_half + min(high, q_half)])
+        if high > q_half:
+            begin = side * p_half + max(low, q_half) - q_half
+            parts.append(wproj_ref[rows, begin : side * p_half + high - q_half])
+        return jnp.concatenate(parts, 1) if len(parts) > 1 else parts[0]
+
+    for k in range(CHUNKS):
+        for side in range(2):
+            core_send[k, :, side * span : (side + 1) * span] = piece(theirs, side, k).astype(b16)
+    pl.semaphore_wait(barrier, len(greeted))
 
     def start(src, dst, sems, device):
         copy = pltpu.make_async_remote_copy(
@@ -332,67 +418,150 @@
         copy.start()
         return copy
 
-    big = start(core_send, core_get, core_sems, partner)
+    bigs = [start(core_send.at[0], core_get.at[0], core_sems.at[0], partner)]
     tiny = start(small_ref, small_core, tiny_sems.at[0], partner)
-    tiny.wait()
-    small_a[...] = small_ref[...] + small_core[...]
-    tiny = start(small_a, small_image, tiny_sems.at[1], image)
-    big.wait()
-
-    def halves(first):
-        q = wqkv_ref[mine, first * q_half : (first + 1) * q_half]
-        p = wproj_ref[mine, first * p_half : (first + 1) * p_half]
-        gq = core_get[:, first * q_half : (first + 1) * q_half]
-        gp = core_get[:, 2 * q_half + first * p_half : 2 * q_half + (first + 1) * p_half]
-        return q + gq.astype(f32), p + gp.astype(f32)
-
-    low, high = halves(0), halves(1)
-    for part, (a, b) in enumerate(zip(low, high)):
-        place = slice(0, q_half) if part == 0 else slice(q_half, q_half + p_half)
-        image_send[:, place] = jnp.where(ba == 0, b, a).astype(b16)
-        image_keep[:, place] = jnp.where(ba == 0, a, b)
-    big = start(image_send, image_get, image_sems, image)
-    tiny.wait()
-    small_b[...] = small_a[...] + small_image[...]
-    tinies = []
-    for step in range(1, peers):
-        tinies.append(start(small_b, small_near.at[step - 1], tiny_sems.at[step + 1], peer(step)[1]))
-    big.wait()
-    total = image_keep[...] + image_get[...].astype(f32)
-    r, c = near_send.shape[1:]
-    split_c = total.shape[1] // c
-    for j in range(peers):
-        row, col = j // split_c * r, j % split_c * c
-        near_send[j] = total[row : row + r, col : col + c].astype(b16)
-    copies = []
-    for step in range(1, peers):
-        other, device = peer(step)
-        copies.append(start(near_send.at[other], near_get.at[step - 1], near_sems.at[step - 1], device))
+    for k in range(1, CHUNKS):
+        bigs.append(start(core_send.at[k], core_get.at[k], core_sems.at[k], partner))
+
+    rows_here, cols_here = cot_ref.shape[:2]
+    shift = window // 2
+    length = window * window
+    edge = shift * window
+    tiles, bands = cols_here // window, rows_here // window
+    halos = []
+    for band in range(bands):
+        size = length if band < bands - 1 else length - edge
+        place = (band * tiles + tiles - 1) * length
+        halos.append(
+            start(
+                d_flat_ref.at[pl.ds(place, size)], side_get.at[pl.ds(band * length, size)],
+                halo_sems.at[len(halos)], (ha, right, ba),
+            )
+        )
+    for tile in range(tiles):
+        place = ((bands - 1) * tiles + tile) * length + length - edge
+        halos.append(
+            start(
+                d_flat_ref.at[pl.ds(place, edge)], row_get.at[tile],
+                halo_sems.at[len(halos)], (down, wa, ba),
+            )
+        )
+    place = bands * tiles * length - edge
+    halos.append(
+        start(
+            d_flat_ref.at[pl.ds(place, edge)], corner_get, halo_sems.at[len(halos)],
+            (down, right, ba),
+        )
+    )
+
+    def to_image(k):
+        low = piece(mine, 0, k) + core_get[k, :, :span].astype(f32)
+        high = piece(mine, 1, k) + core_get[k, :, span:].astype(f32)
+        image_send[k] = jnp.where(ba == 0, high, low).astype(b16)
+        image_keep[k] = jnp.where(ba == 0, low, high)
+        return start(image_send.at[k], image_get.at[k], image_sems.at[k], image)
+
+    images = []
+    for k in range(CHUNKS):
+        bigs[k].wait()
+        images.append(to_image(k))
+        if k == 0:
+            tiny.wait()
+            small_a[...] = small_ref[...] + small_core[...]
+            tiny = start(small_a, small_image, tiny_sems.at[1], image)
+
+    r, c = near_send.shape[2:]
+    split_c = span // c
+
+    def place_of(j):
+        return j // split_c * r, j % split_c * c
+
+    nears, tinies = [], []
+    for k in range(CHUNKS):
+        images[k].wait()
+        total = image_keep[k] + image_get[k].astype(f32)
+        for j in range(peers):
+            row, col = place_of(j)
+            near_send[k, j] = total[row : row + r, col : col + c].astype(b16)
+        copies = []
+        for step in range(1, peers):
+            other, device = peer(step)
+            copies.append(
+                start(
+                    near_send.at[k, other], near_get.at[k, step - 1], near_sems.at[k, step - 1], device
+                )
+            )
+        nears.append(copies)
+        if k == 0:
+            tiny.wait()
+            small_b[...] = small_a[...] + small_image[...]
+            for step in range(1, peers):
+                tinies.append(
+                    start(small_b, small_near.at[step - 1], tiny_sems.at[step + 1], peer(step)[1])
+                )
+
+    alls = []
+    for k in range(CHUNKS):
+        for copy in nears[k]:
+            copy.wait()
+        total = near_send[k, me].astype(f32)
+        for step in range(1, peers):
+            total = total + near_get[k, step - 1].astype(f32)
+        own[k] = total.astype(b16)
+        whole[k, me] = own[k]
+        alls.append(
+            [
+                start(own.at[k], whole.at[k, me], all_sems.at[k, step - 1], peer(step)[1])
+                for step in range(1, peers)
+            ]
+        )
+
     for copy in tinies:
         copy.wait()
     small = small_b[...]
     for step in range(1, peers):
         small = small + small_near[step - 1]
     small_out[...] = small
-    for copy in copies:
+
+    for copy in halos:
         copy.wait()
-    total = near_send[me].astype(f32)
-    for step in range(1, peers):
-        total = total + near_get[step - 1].astype(f32)
-    own[...] = total.astype(b16)
-    whole[me] = own[...]
-    copies = []
-    for step in range(1, peers):
-        _, device = peer(step)
-        copies.append(start(own, whole.at[me], all_sems.at[step - 1], device))
-    for copy in copies:
-        copy.wait()
-    last = start(whole, core_all, last_sems, partner)
-
-    def put(source, first):
+    depth_here = cot_ref.shape[2]
+    later = lax.broadcasted_iota(jnp.int32, (1, window, depth_here), 1) >= shift
+
+    def moved_tile(tile, first, count):
+        parts = []
+        for band in range(bands):
+            begin, end = max(first, band * window), min(first + count, (band + 1) * window)
+            if begin < end:
+                source, base = d_flat_ref, (band * tiles + tile) * length
+                if tile < 0:
+                    source, base = side_get, band * length
+                low = base + (begin - band * window) * window
+                parts.append(source[low : low + (end - begin) * window, :])
+        value = [part.astype(f32).reshape(-1, window, depth_here) for part in parts]
+        return jnp.concatenate(value, 0)
+
+    def above_tile(tile):
+        value = corner_get[...] if tile < 0 else row_get[tile]
+        return value.astype(f32).reshape(shift, window, depth_here)
+
+    body = rows_here - shift
+    for first in range(0, body, shift):
+        grads = [moved_tile(tile, first, shift) for tile in range(-1, tiles)]
+        wide = [jnp.where(later, grads[n + 1], grads[n]) for n in range(tiles)]
+        wide = jnp.concatenate([x[:, None] for x in wide], 1).reshape(shift, cols_here, depth_here)
+        there = slice(first + shift, first + 2 * shift)
+        tokens_out[there] = (cot_ref[there].astype(f32) + wide).astype(b16)
+    grads = [above_tile(tile) for tile in range(-1, tiles)]
+    wide = [jnp.where(later, grads[n + 1], grads[n]) for n in range(tiles)]
+    wide = jnp.concatenate([x[:, None] for x in wide], 1).reshape(shift, cols_here, depth_here)
+    tokens_out[:shift] = (cot_ref[:shift].astype(f32) + wide).astype(b16)
+
+    def put(source, k, first):
         for j in range(peers):
-            row, col = j // split_c * r, j % split_c * c
-            block = source[j].astype(f32)
+            row, col = place_of(j)
+            col = col + k * span
+            block = source[k, j].astype(f32)
             rows = pl.ds(pl.multiple_of(first * half + row, 8), r)
             q_part = max(0, min(c, q_half - col))
             if q_part > 0:
@@ -401,58 +570,75 @@
                 begin = col + q_part - q_half
                 proj_out[rows, begin : begin + c - q_part] = block[:, q_part:]
 
-    put(whole, core)
-    last.wait()
-    put(core_all, 1 - core)
-
-
-def reduce_all(d_wqkv, d_wproj, small):
+    lasts = []
+    for k in range(CHUNKS):
+        for copy in alls[k]:
+            copy.wait()
+        lasts.append(start(whole.at[k], core_all.at[k], last_sems.at[k], partner))
+        put(whole, k, core)
+    for k in range(CHUNKS):
+        lasts[k].wait()
+        put(core_all, k, 1 - core)
+
+
+def reduce_all(d_wqkv, d_wproj, small, d_flat, cotangent, window):
     size_h, size_w = lax.axis_size("ha"), lax.axis_size("wa")
     peers = size_h // 2 * size_w
     depth = d_wqkv.shape[0]
     half = depth // 2
-    cols = (d_wqkv.shape[1] + d_wproj.shape[1]) // 2
+    cols = (d_wqkv.shape[1] + d_wproj.shape[1]) // 2 // CHUNKS
     split_c = 2
     r, c = half * split_c // peers, cols // split_c
     f32, b16 = jnp.float32, jnp.bfloat16
     tiny = small.shape
-    return pl.pallas_call(
-        functools.partial(reduce_kernel, (size_h, size_w)),
+    _, rows_here, cols_here, channels = cotangent.shape
+    tiles, bands = cols_here // window, rows_here // window
+    length = window * window
+    edge = length // 2
+    quick, near = pltpu.SemaphoreType.DMA((CHUNKS, 2)), pltpu.SemaphoreType.DMA((CHUNKS, peers - 1, 2))
+    *sums, d_tokens = pl.pallas_call(
+        functools.partial(reduce_kernel, (size_h, size_w), window),
         out_shape=[
             jax.ShapeDtypeStruct((depth, d_wqkv.shape[1] // 2), f32),
             jax.ShapeDtypeStruct((depth, d_wproj.shape[1] // 2), f32),
             jax.ShapeDtypeStruct(tiny, f32),
+            jax.ShapeDtypeStruct((rows_here, cols_here, channels), b16),
         ],
-        in_specs=[VMEM] * 3,
-        out_specs=[VMEM] * 3,
+        in_specs=[VMEM] * 5,
+        out_specs=[VMEM] * 4,
         scratch_shapes=[
-            pltpu.VMEM((half, 2 * cols), b16),
-            pltpu.VMEM((half, 2 * cols), b16),
-            pltpu.VMEM((half, cols), f32),
-            pltpu.VMEM((half, cols), b16),
-            pltpu.VMEM((half, cols), b16),
-            pltpu.VMEM((peers, r, c), b16),
-            pltpu.VMEM((peers - 1, r, c), b16),
-            pltpu.VMEM((r, c), b16),
-            pltpu.VMEM((peers, r, c), b16),
-            pltpu.VMEM((peers, r, c), b16),
+            pltpu.VMEM((CHUNKS, half, 2 * cols), b16),
+            pltpu.VMEM((CHUNKS, half, 2 * cols), b16),
+            pltpu.VMEM((CHUNKS, half, cols), f32),
+            pltpu.VMEM((CHUNKS, half, cols), b16),
+            pltpu.VMEM((CHUNKS, half, cols), b16),
+            pltpu.VMEM((CHUNKS, peers, r, c), b16),
+            pltpu.VMEM((CHUNKS, peers - 1, r, c), b16),
+            pltpu.VMEM((CHUNKS, r, c), b16),
+            pltpu.VMEM((CHUNKS, peers, r, c), b16),
+            pltpu.VMEM((CHUNKS, peers, r, c), b16),
             pltpu.VMEM(tiny, f32),
             pltpu.VMEM(tiny, f32),
             pltpu.VMEM(tiny, f32),
             pltpu.VMEM(tiny, f32),
             pltpu.VMEM((peers - 1, *tiny), f32),
-            pltpu.SemaphoreType.DMA((2,)),
-            pltpu.SemaphoreType.DMA((2,)),
-            pltpu.SemaphoreType.DMA((peers - 1, 2)),
-            pltpu.SemaphoreType.DMA((peers - 1, 2)),
-            pltpu.SemaphoreType.DMA((2,)),
+            pltpu.VMEM((bands * length, channels), b16),
+            pltpu.VMEM((tiles, edge, channels), b16),
+            pltpu.VMEM((edge, channels), b16),
+            quick,
+            quick,
+            near,
+            near,
+            quick,
             pltpu.SemaphoreType.DMA((peers + 1, 2)),
+            pltpu.SemaphoreType.DMA((bands + tiles + 1, 2)),
         ],
         compiler_params=pltpu.CompilerParams(
             collective_id=0, has_side_effects=True, vmem_limit_bytes=48 * 2**20
         ),
         name="reduce_all",
-    )(d_wqkv, d_wproj, small)
+    )(d_wqkv, d_wproj, small, d_flat, cotangent.reshape(rows_here, cols_here, channels))
+    return (*sums, d_tokens.reshape(cotangent.shape))
 
 
 def can_reduce(d_wqkv):
@@ -477,15 +663,6 @@
     return full[:heads, :entries], flat[:heads], flat[heads : heads + depth]
 
 
-def shift_in(tokens, cotangent, shift):
-    stacked = jnp.stack([tokens, cotangent])
-    below = from_behind(stacked[:, :, :shift], "ha", -1)
-    tall = jnp.concatenate([stacked[:, :, shift:], below], 2)
-    beside = from_behind(tall[:, :, :, :shift], "wa", -1)
-    moved = jnp.concatenate([tall[:, :, :, shift:], beside], 3)
-    return (moved[0], moved[1])
-
-
 def shift_out(grads, shift):
     rows = grads.shape[1]
     cols = grads.shape[2]
@@ -501,19 +678,21 @@
     shift = WIN // 2
     height = rows * lax.axis_size("ha")
     width = cols * lax.axis_size("wa")
-    row_base = lax.axis_index("ha") * rows
-    col_base = lax.axis_index("wa") * cols
     params = (w_qkv, w_proj, table_logits, logit_scale, gain)
-    moved, moved_grad = shift_in(tokens, cotangent, shift)
-    d_moved, parts = local_grads(moved, moved_grad, row_base, col_base, height, width, WIN, params)
-    back = shift_out(d_moved, shift)
-    d_tokens = (cotangent.astype(jnp.float32) + back.astype(jnp.float32)).astype(jnp.bfloat16)
+    flat, grad_flat = shift_in(tokens, cotangent, WIN)
+    d_flat, parts = local_grads(flat, grad_flat, cols, height, width, WIN, params)
     d_wqkv, d_wproj, d_table, d_scale, d_gain = parts
     if can_reduce(d_wqkv):
         small = pack_small(d_table, d_scale, d_gain)
-        half_qkv, half_proj, small = reduce_all(d_wqkv, d_wproj, small)
+        half_qkv, half_proj, small, d_tokens = reduce_all(
+            d_wqkv, d_wproj, small, d_flat, cotangent, WIN
+        )
         d_table, d_scale, d_gain = unpack_small(small, *d_table.shape, d_gain.shape[0])
     else:
+        turned = jnp.roll(d_flat.reshape(-1, WIN, d_flat.shape[1]), -shift, 1)
+        turned = turned.reshape(-1, WIN * WIN, d_flat.shape[1])
+        back = shift_out(from_windows(turned, tokens.shape[0], rows, cols, WIN), shift)
+        d_tokens = (cotangent.astype(jnp.float32) + back.astype(jnp.float32)).astype(jnp.bfloat16)
         half_qkv, half_proj = (
             lax.psum_scatter(d_wqkv.astype(jnp.bfloat16), "ba", scatter_dimension=1, tiled=True).astype(
                 jnp.float32

time: 87.9 us -> 88.3 us (level)
  Pallas kernels: 59.1 us -> 70.2 us
  starting transfers between devices: 8.16 us -> 0 us
  waiting for transfers between devices: 5.02 us -> 0 us
  local copies, waits for them, and re-layouts: 8.47 us -> 12.7 us
  other arithmetic: 3.52 us -> 1.76 us
    pallas_call x1 -> x2, Pallas kernels: 29.4 us -> 40.5 us  [the longest x1 30.3 us: reduce_all(): pl.pallas_call(functools.partial(reduce_kernel, (size_h, size_w), window)...]
    ppermute x4 -> x0, starting transfers between devices: 8.16 us -> none  [from_behind(): return lax.ppermute(block, axis, route)]
    unnamed x33 -> x30, local copies, waits for them, and re-layouts: 3.85 us -> 9.33 us
    ppermute x4 -> x0, waiting for transfers between devices: 5.02 us -> none  [from_behind(): return lax.ppermute(block, axis, route)]
    another operation x4 -> x2, other arithmetic: 1.83 us -> 0.79 us  [the longest x2 1.05 us: shift_in(): stacked = jnp.stack([tokens, cotangent])]
    reshape x1, local copies, waits for them, and re-layouts: 1.15 us -> 0.14 us  [local_grads(): heads_bias = heads_bias.reshape(heads, length * length)]
    convert_element_type x1 -> x0, other arithmetic: 0.91 us -> none  [shards(): (cotangent.astype(jnp.float32) + back.astype(jnp.float32)).astype(jnp.bfl...]
  transfers between devices with their start and end apart: 4 -> 0, of which waited for: 2 -> 0; matrix products, arithmetic and copies ran while one was open for 11% -> 0% of each run, Pallas kernels for 34% -> 0%
where the time goes in v2:
time: 88.3 us; the launch traced here: 87.9 us
  Pallas kernels  70.2 us (80%)
  local copies, waits for them, and re-layouts  12.7 us (14%)
  matrix products  2.26 us (3%)
  other arithmetic  1.76 us (2%)
    pallas_call x1, Pallas kernels, reduce_all(): pl.pallas_call(functools.partial(reduce_kernel, (size_h, size_w), window)...  30.3 us
    pallas_call x1, Pallas kernels, local_grads(): pl.pallas_call(functools.partial(local_kernel, cols // window, height, wi...  29.8 us
    pallas_call x1, Pallas kernels, shift_in(): pl.pallas_call(functools.partial(shift_in_kernel, lax.axis_size('ha'), la...  10.2 us
    unnamed x30, local copies, waits for them, and re-layouts  9.33 us

profile of v2, /device:TPU:0, one launch (start us, length us, event | category | flops | bytes accessed | tf_op | source)
XLA Modules:
  0.0 87.9 jit_solution(17286149371090097598)
XLA Ops:
  0.6 0.7 minimum_exponential_fusion
  1.4 0.7 reshape.67.gain_ref
  2.2 0.7 reduce-precision_convert_fusion.3
  3.0 1.5 %fusion.1 = f32[36,4096]{1,0:T(8,128)S(1)} fusion(s32[4096]{0:T(1024)} %constant.13.clone, bf16[12,225]{1,0:T(8,128)(2,1)S(1)} %get-tuple-element.52, bf16[12,225]{1,0:T(8,128)(2,1)S(1)} %get-tuple-element.53, bf16[12,225]{1,0:T(8,128)(2,1)S(1)} %get-tuple-element.51), kind=kOutput, calls=%fused_computation.2 | convolution fusion | flops 67325400 | bytes 622408 | tf_op jit(solution)/shard_map/dot_general | solution.py:242
  4.6 0.2 reshape.64
  4.8 0.3 copy.20
  5.0 0.3 reshape.65.bias_ref
  5.3 0.2 copy-done
  5.6 10.2 %shift_in.1 = (bf16[512,384]{1,0:T(8,128)(2,1)S(1)}, bf16[512,384]{1,0:T(8,128)(2,1)S(1)}) custom-call(bf16[16,32,384]{2,1,0:T(8,128)(2,1)S(1)} %bitcast.15, bf16[16,32,384]{2,1,0:T(8,128)(2,1)S(1)} %bitcast.13), custom_call_target="tpu_custom_call" | custom-call | tf_op jit(solution)/shard_map/shift_in/pallas_call | solution.py:340
  15.9 1.2 %copy-done.7 = bf16[384,1152]{1,0:T(8,128)(2,1)S(1)} copy-done((bf16[384,1152]{1,0:T(8,128)(2,1)S(1)}, bf16[384,1152]{1,0:T(8,128)(2,1)}, u32[]{:S(2)}) %copy-start.7) | copy-done | bytes 884760
  17.0 29.8 %local_grads.1 = (bf16[512,384]{1,0:T(8,128)(2,1)S(1)}, f32[384,1152]{1,0:T(8,128)S(1)}, f32[384,384]{1,0:T(8,128)S(1)}, f32[3,64,256]{2,1,0:T(8,128)S(1)}, f32[...) custom-call(bf16[512,384]{1,0:T(8,128)(2,1)S(1)} %get-tuple-element.18.flat_ref, ...), custom_call_target="tpu_custom_call" | custom-call | flops 4000000000 | bytes 8000000 | tf_op jit(solution)/shard_map/local_grads/pallas_call | solution.py:246
  46.8 0.8 copy-done.1
  48.0 0.2 reshape.68
  48.5 0.8 fusion
  49.4 1.1 %copy-done.2 = f32[384,384]{1,0:T(8,128)S(1)} copy-done((f32[384,384]{1,0:T(8,128)S(1)}, f32[384,384]{1,0:T(8,128)}, u32[]{:S(2)}) %copy-start.2) | copy-done | bytes 589848
  50.5 30.3 %reduce_all.1 = (f32[384,576]{1,0:T(8,128)S(1)}, f32[384,192]{1,0:T(8,128)S(1)}, f32[16,256]{1,0:T(8,128)S(1)}, bf16[16,32,384]{2,1,0:T(8,128)(2,1)S(1)}) custom-call(f32[384,1152]{1,0:T(8,128)S(1)} %get-tuple-element.20.wqkv_ref, f32[384,384]{1,0:T(8,128)S(1)} %copy-done.2, f32[16,256]{1,0:T(8,128)S(1)} %pad.14.small_ref, ...), custom_call_target="tpu_custom_call" | custom-call | tf_op jit(solution)/shard_map/reduce_all/pallas_call | solution.py:599
  80.8 0.7 copy-done.4
  81.5 0.7 copy-done.6
  82.3 0.5 slice.14
  82.8 0.6 slice.15
  83.4 1.9 %copy.23 = f32[384,192]{0,1:T(8,128)} copy(f32[384,192]{1,0:T(8,128)} %copy-done.6) | data formatting | bytes 589824
  85.3 1.2 %copy.22 = f32[384,576]{0,1:T(8,128)} copy(f32[384,576]{1,0:T(8,128)S(1)} %get-tuple-element.43) | data formatting | bytes 1769472
  86.5 0.7 copy.29
  87.3 0.6 copy.30
  (41 shorter events, 1.2 us)
Async XLA Ops:
  4.5 1.0 %copy-start = (bf16[1,16,32,384]{3,2,1,0:T(8,128)(2,1)S(1)}, bf16[1,16,32,384]{3,2,1,0:T(8,128)(2,1)}, u32[]{:S(2)}) copy-start(bf16[1,16,32,384]{3,2,1,0:T(8,128)(2,1)} %param.9) | copy-start | bytes 1179652
  4.5 1.1 %copy-start.3 = (bf16[1,16,32,384]{3,2,1,0:T(8,128)(2,1)S(1)}, bf16[1,16,32,384]{3,2,1,0:T(8,128)(2,1)}, u32[]{:S(2)}) copy-start(bf16[1,16,32,384]{3,2,1,0:T(8,128)(2,1)} %param.8) | copy-start | bytes 1179652
  4.5 11.3 %copy-start.8 = (bf16[384,384]{1,0:T(8,128)(2,1)S(1)}, bf16[384,384]{1,0:T(8,128)(2,1)}, u32[]{:S(2)}) copy-start(bf16[384,384]{1,0:T(8,128)(2,1)} %w_proj_ref.1) | copy-start | bytes 884740
  15.8 1.2 %copy-start.7 = (bf16[384,1152]{1,0:T(8,128)(2,1)S(1)}, bf16[384,1152]{1,0:T(8,128)(2,1)}, u32[]{:S(2)}) copy-start(bf16[384,1152]{1,0:T(8,128)(2,1)} %w_qkv_ref.1) | copy-start | bytes 2654212
  17.0 30.9 %copy-start.10 = (f32[12]{0:T(128)S(1)}, f32[12]{0:T(128)}, u32[]{:S(2)}) copy-start(f32[12]{0:T(128)} %param.13) | copy-start | bytes 148
  46.8 0.8 copy-start.1
  47.6 0.9 %copy-start.11 = (s32[4096]{0:T(1024)S(1)}, s32[4096]{0:T(1024)}, u32[]{:S(2)}) copy-start(s32[4096]{0:T(1024)} %constant.13.clone) | copy-start | bytes 49156
  48.3 1.1 %copy-start.9 = (f32[12,225]{1,0:T(8,128)S(1)}, f32[12,225]{1,0:T(8,128)}, u32[]{:S(2)}) copy-start(f32[12,225]{1,0:T(8,128)} %param.12) | copy-start | bytes 32404
  49.4 1.1 %copy-start.2 = (f32[384,384]{1,0:T(8,128)S(1)}, f32[384,384]{1,0:T(8,128)}, u32[]{:S(2)}) copy-start(f32[384,384]{1,0:T(8,128)} %copy-done.1) | copy-start | bytes 1769476
  80.7 0.7 copy-start.4
  81.5 0.7 copy-start.6
  82.2 4.3 %copy-start.5 = (bf16[16,32,384]{2,1,0:T(8,128)(2,1)S(1)}, bf16[16,32,384]{2,1,0:T(8,128)(2,1)}, u32[]{:S(2)}) copy-start(bf16[16,32,384]{2,1,0:T(8,128)(2,1)} %copy-done.4) | copy-start | bytes 1179652

commit v3 on v1

--- a/solution.py
+++ b/solution.py
@@ -198,9 +198,9 @@
             query_wide = lax.rsqrt(query_sum + 1.0)
             query_inv = lax.rsqrt(mxu_fine(jnp.square(query32), lane_lane, NN) + 1.0)
             key_inv = lax.rsqrt(mxu_fine(jnp.square(key32), lane_lane, NN) + 1.0)
-            d_unit_q = mxu_fine(scaled_scores * key_row_inv(tall), tall, NN)
+            d_unit_q = mxu((scaled_scores * key_row_inv(tall)).astype(jnp.bfloat16), tall, NN)
             d_unit_k = gather_heads(
-                mxu_fine(scaled_scores * query_wide, query, TN), head_dim, length
+                mxu((scaled_scores * query_wide).astype(jnp.bfloat16), query, TN), head_dim, length
             )
             unit_q, unit_k = query32 * query_inv, key32 * key_inv
             d_query = query_inv * (d_unit_q - unit_q * mxu_fine(unit_q * d_unit_q, lane_lane, NN))

time: 87.9 us -> 88.5 us (level)
  transfers between devices with their start and end apart: 4 -> 4, of which waited for: 2 -> 2; matrix products, arithmetic and copies ran while one was open for 11% -> 11% of each run, Pallas kernels for 34% -> 33%
where the time goes in v3:
time: 88.5 us; the launch traced here: 88.1 us
  Pallas kernels  59.7 us (67%)
  local copies, waits for them, and re-layouts  8.47 us (10%)
  starting transfers between devices  8.16 us (9%)
  waiting for transfers between devices  5.02 us (6%)
  other arithmetic  3.52 us (4%)
  matrix products  2.26 us (3%)
  between operations  0.98 us (1%)
    pallas_call x1, Pallas kernels, local_grads(): pl.pallas_call(functools.partial(local_kernel, cols // window, height, wi...  30.4 us
    pallas_call x1, Pallas kernels, reduce_all(): pl.pallas_call(functools.partial(reduce_kernel, (size_h, size_w)), out_sh...  29.4 us
    ppermute x4, starting transfers between devices, from_behind(): return lax.ppermute(block, axis, route)  8.16 us
    ppermute x4, waiting for transfers between devices, from_behind(): return lax.ppermute(block, axis, route)  5.02 us
    unnamed x33, local copies, waits for them, and re-layouts  3.85 us
  transfers between devices with their start and end apart: 4, of which 2 were waited for; matrix products, arithmetic and copies ran while one was open for 11% of the time, Pallas kernels for 33%

profile of v3, /device:TPU:0, one launch (start us, length us, event | category | flops | bytes accessed | tf_op | source)
XLA Modules:
  0.0 88.1 jit_solution(6605527106119458258)
XLA Ops:
  0.7 1.0 %pad_maximum_fusion.2 = bf16[2,1,4,32,384]{4,3,2,1,0:T(8,128)(2,1)S(1)} fusion(bf16[1,1,16,32,384]{4,3,2,1,0:T(8,128)(2,1)} %bitcast.32, bf16[1,1,16,32,384]{4,3,2,1,0:T(8,128)(2,1)} %bitcast.38), kind=kLoop, calls=%fused_computation.27 | loop fusion | flops 98304 | bytes 983040 | tf_op jit(solution)/shard_map/stack | solution.py:481
  1.6 4.6 %collective-permute-start = (bf16[2,1,4,32,384]{4,3,2,1,0:T(8,128)(2,1)S(1)}, bf16[2,1,4,32,384]{4,3,2,1,0:T(8,128)(2,1)S(1)}, u32[]{:S(2)}, u32[]{:S(2)}) collective-permute-start(bf16[2,1,4,32,384]{4,3,2,1,0:T(8,128)(2,1)S(1)} %pad_maximum_fusion.2), channel_id=1, source_target_pairs={{4,0},{8,4},{12,8},{16,12},{20,16},{24,20},{28,24},{0,28},{5,1},{9... | collective-permute-start | bytes 589832 | tf_op jit(solution)/shard_map/ppermute | solution.py:25
  6.2 0.7 reduce-precision_convert_fusion.3
  6.9 1.5 %fusion.1 = f32[36,4096]{1,0:T(8,128)S(1)} fusion(s32[4096]{0:T(1024)} %constant.13.clone, bf16[12,225]{1,0:T(8,128)(2,1)S(1)} %get-tuple-element.48, bf16[12,225]{1,0:T(8,128)(2,1)S(1)} %get-tuple-element.49, bf16[12,225]{1,0:T(8,128)(2,1)S(1)} %get-tuple-element.47), kind=kOutput, calls=%fused_computation.2 | convolution fusion | flops 67325400 | bytes 622408 | tf_op jit(solution)/shard_map/dot_general | solution.py:251
  9.0 0.3 copy.28
  9.3 0.3 reshape.84.bias_ref
  10.0 1.6 %collective-permute-start.1 = (bf16[2,1,16,4,384]{4,3,2,1,0:T(4,128)(2,1)S(1)}, bf16[2,1,16,4,384]{4,3,2,1,0:T(4,128)(2,1)S(1)}, u32[]{:S(2)}, u32[]{:S(2)}) collective-permute-start(bf16[2,1,16,4,384]{4,3,2,1,0:T(4,128)(2,1)S(1)} %pad_maximum_fusion.4), channel_id=1, source_target_pairs={{2,0},{0,2},{3,1},{1,3},{6,4},{4,6},{7,5},{5,7},{10,8},{8,10},{11,... | collective-permute-start | bytes 294920 | tf_op jit(solution)/shard_map/ppermute | solution.py:25
  11.6 0.2 slice_maximum_fusion
  11.8 2.8 %collective-permute-done.1 = bf16[2,1,16,4,384]{4,3,2,1,0:T(4,128)(2,1)S(1)} collective-permute-done((bf16[2,1,16,4,384]{4,3,2,1,0:T(4,128)(2,1)S(1)}, bf16[2,1,16,4,384]{4,3,2,1,0:T(4,128)(2,1)S(1)}, u32[]{:S(2)}, u32[]{:S(2)}) %collective-permute-start.1) | collective-permute-done | bytes 98336 | tf_op jit(solution)/shard_map/ppermute | solution.py:25
  14.9 30.4 %local_grads.1 = (bf16[512,384]{1,0:T(8,128)(2,1)S(1)}, f32[384,1152]{1,0:T(8,128)S(1)}, f32[384,384]{1,0:T(8,128)S(1)}, f32[3,64,256]{2,1,0:T(8,128)S(1)}, f32[...) custom-call(bf16[512,384]{1,0:T(8,128)(2,1)S(1)} %bitcast.26, bf16[512,384]{1,0:T(8,128)(2,1)S(1)} %bitcast.25, ...), custom_call_target="tpu_custom_call" | custom-call | flops 4000000000 | bytes 8000000 | tf_op jit(solution)/shard_map/local_grads/pallas_call | solution.py:255
  45.8 1.6 %collective-permute-start.2 = (bf16[1,16,4,384]{3,2,1,0:T(4,128)(2,1)S(1)}, bf16[1,16,4,384]{3,2,1,0:T(4,128)(2,1)S(1)}, u32[]{:S(2)}, u32[]{:S(2)}) collective-permute-start(bf16[1,16,4,384]{3,2,1,0:T(4,128)(2,1)S(1)} %slice.62), channel_id=1, source_target_pairs={{2,0},{0,2},{3,1},{1,3},{6,4},{4,6},{7,5},{5,7},{10,8},{8,10},{11,... | collective-permute-start | bytes 147464 | tf_op jit(solution)/shard_map/ppermute | solution.py:25
  47.6 0.8 copy.35
  48.4 1.1 %reshape.89 = f32[12,4096]{1,0:T(8,128)S(1)} reshape(f32[3,4,64,64]{3,2,1,0:T(8,128)} %bitcast.35) | data formatting | bytes 393216 | tf_op jit(solution)/shard_map/reshape | solution.py:282
  49.6 0.8 fusion
  50.5 29.4 %reduce_all.1 = (f32[384,576]{1,0:T(8,128)S(1)}, f32[384,192]{1,0:T(8,128)S(1)}, f32[16,256]{1,0:T(8,128)S(1)}) custom-call(f32[384,1152]{1,0:T(8,128)S(1)} %get-tuple-element.16.wqkv_ref, f32[384,384]{1,0:T(8,128)S(1)} %get-tuple-element.17.wproj_ref, f32[16,256]{1,0:T(8,128)S(1)} %pad.14.small_ref), custom_call_target="tpu_custom_call" | custom-call | tf_op jit(solution)/shard_map/reduce_all/pallas_call | solution.py:419
  79.9 0.7 copy-done
  80.7 0.4 collective-permute-start.3
  81.1 0.5 slice.54
  81.7 0.6 slice.55
  82.3 1.2 %copy.31 = f32[384,576]{0,1:T(8,128)} copy(f32[384,576]{1,0:T(8,128)S(1)} %get-tuple-element.37) | data formatting | bytes 1769472
  83.5 0.9 copy.32
  84.4 2.2 %collective-permute-done.3 = bf16[1,4,32,384]{3,2,1,0:T(8,128)(2,1)S(1)} collective-permute-done((bf16[1,4,32,384]{3,2,1,0:T(8,128)(2,1)S(1)}, bf16[1,4,32,384]{3,2,1,0:T(8,128)(2,1)S(1)}, u32[]{:S(2)}, u32[]{:S(2)}) %collective-permute-start.3) | collective-permute-done | bytes 98336 | tf_op jit(solution)/shard_map/ppermute | solution.py:25
  86.6 0.9 %add_convert_fusion = bf16[1,16,32,384]{3,2,1,0:T(8,128)(2,1)} fusion(bf16[1,16,32,384]{3,2,1,0:T(8,128)(2,1)S(1)} %copy-done.8, bf16[1,16,28,384]{3,2,1,0:T(8,128)(2,1)S(1)} %bitcast.31, bf16[1,16,4,384]{3,2,1,0:T(4,128)(2,1)S(1)} %collective-permute-done.2, bf16[1,4,32,384]{3,2,1,0:T(8,128)(2,1)S(1)} %collective-permute-done.3), kind=kLoop, calls=%fused_computation.10 | loop fusion | flops 1769472 | bytes 1277952 | tf_op jit(solution)/shard_map/convert_element_type | solution.py:510
  87.5 0.6 copy.37
  (62 shorter events, 2.1 us)
Async XLA Ops:
  0.6 7.8 %copy-start.12 = (f32[12]{0:T(128)S(1)}, f32[12]{0:T(128)}, u32[]{:S(2)}) copy-start(f32[12]{0:T(128)} %param.13) | copy-start | bytes 148
  0.6 7.9 %copy-start.11 = (f32[384]{0:T(512)S(1)}, f32[384]{0:T(512)}, u32[]{:S(2)}) copy-start(f32[384]{0:T(512)} %param.14) | copy-start | bytes 4612
  1.6 8.3 %collective-permute-start = (bf16[2,1,4,32,384]{4,3,2,1,0:T(8,128)(2,1)S(1)}, bf16[2,1,4,32,384]{4,3,2,1,0:T(8,128)(2,1)S(1)}, u32[]{:S(2)}, u32[]{:S(2)}) collective-permute-start(bf16[2,1,4,32,384]{4,3,2,1,0:T(8,128)(2,1)S(1)} %pad_maximum_fusion.2), channel_id=1, source_target_pairs={{4,0},{8,4},{12,8},{16,12},{20,16},{24,20},{28,24},{0,28},{5,1},{9... | collective-permute-start | bytes 589832 | tf_op jit(solution)/shard_map/ppermute | solution.py:25
  8.7 1.0 %copy-start.7 = (bf16[1,16,32,384]{3,2,1,0:T(8,128)(2,1)S(1)}, bf16[1,16,32,384]{3,2,1,0:T(8,128)(2,1)}, u32[]{:S(2)}) copy-start(bf16[1,16,32,384]{3,2,1,0:T(8,128)(2,1)} %param.9) | copy-start | bytes 1179652
  8.8 1.1 %copy-start.9 = (bf16[1,16,32,384]{3,2,1,0:T(8,128)(2,1)S(1)}, bf16[1,16,32,384]{3,2,1,0:T(8,128)(2,1)}, u32[]{:S(2)}) copy-start(bf16[1,16,32,384]{3,2,1,0:T(8,128)(2,1)} %param.8) | copy-start | bytes 1179652
  10.0 4.7 %collective-permute-start.1 = (bf16[2,1,16,4,384]{4,3,2,1,0:T(4,128)(2,1)S(1)}, bf16[2,1,16,4,384]{4,3,2,1,0:T(4,128)(2,1)S(1)}, u32[]{:S(2)}, u32[]{:S(2)}) collective-permute-start(bf16[2,1,16,4,384]{4,3,2,1,0:T(4,128)(2,1)S(1)} %pad_maximum_fusion.4), channel_id=1, source_target_pairs={{2,0},{0,2},{3,1},{1,3},{6,4},{4,6},{7,5},{5,7},{10,8},{8,10},{11,... | collective-permute-start | bytes 294920 | tf_op jit(solution)/shard_map/ppermute | solution.py:25
  11.8 3.1 %copy-start.2 = (bf16[384,1152]{1,0:T(8,128)(2,1)S(1)}, bf16[384,1152]{1,0:T(8,128)(2,1)}, u32[]{:S(2)}) copy-start(bf16[384,1152]{1,0:T(8,128)(2,1)} %w_qkv_ref.1) | copy-start | bytes 2654212
  11.8 3.1 %copy-start.3 = (bf16[384,384]{1,0:T(8,128)(2,1)S(1)}, bf16[384,384]{1,0:T(8,128)(2,1)}, u32[]{:S(2)}) copy-start(bf16[384,384]{1,0:T(8,128)(2,1)} %w_proj_ref.1) | copy-start | bytes 884740
  45.3 4.3 %copy-start.13 = (s32[4096]{0:T(1024)S(1)}, s32[4096]{0:T(1024)}, u32[]{:S(2)}) copy-start(s32[4096]{0:T(1024)} %constant.13.clone) | copy-start | bytes 49156
  45.4 5.1 %copy-start.4 = (bf16[1,2,8,4,8,384]{5,4,3,2,1,0:T(8,128)(2,1)}, bf16[1,2,8,4,8,384]{5,4,3,2,1,0:T(8,128)(2,1)S(1)}, u32[]{:S(2)}) copy-start(bf16[1,2,8,4,8,384]{5,4,3,2,1,0:T(8,128)(2,1)S(1)} %copy.29) | copy-start | bytes 1179652
  45.8 34.8 %collective-permute-start.2 = (bf16[1,16,4,384]{3,2,1,0:T(4,128)(2,1)S(1)}, bf16[1,16,4,384]{3,2,1,0:T(4,128)(2,1)S(1)}, u32[]{:S(2)}, u32[]{:S(2)}) collective-permute-start(bf16[1,16,4,384]{3,2,1,0:T(4,128)(2,1)S(1)} %slice.62), channel_id=1, source_target_pairs={{2,0},{0,2},{3,1},{1,3},{6,4},{4,6},{7,5},{5,7},{10,8},{8,10},{11,... | collective-permute-start | bytes 147464 | tf_op jit(solution)/shard_map/ppermute | solution.py:25
  48.4 2.1 %copy-start.10 = (f32[12,225]{1,0:T(8,128)S(1)}, f32[12,225]{1,0:T(8,128)}, u32[]{:S(2)}) copy-start(f32[12,225]{1,0:T(8,128)} %param.12) | copy-start | bytes 32404
  50.5 30.2 %copy-start.5 = (bf16[1,2,8,4,8,384]{5,4,3,2,1,0:T(8,128)(2,1)S(1)}, bf16[1,2,8,4,8,384]{5,4,3,2,1,0:T(8,128)(2,1)}, u32[]{:S(2)}) copy-start(bf16[1,2,8,4,8,384]{5,4,3,2,1,0:T(8,128)(2,1)} %copy-done.4) | copy-start | bytes 1179652
  79.9 0.7 copy-start
  80.6 6.0 %copy-start.6 = (bf16[1,2,8,4,8,384]{5,4,3,2,1,0:T(8,128)(2,1)S(1)}, bf16[1,2,8,4,8,384]{5,4,3,2,1,0:T(8,128)(2,1)}, u32[]{:S(2)}) copy-start(bf16[1,2,8,4,8,384]{5,4,3,2,1,0:T(8,128)(2,1)} %copy-done.4) | copy-start | bytes 1179652
  80.7 6.0 %copy-start.8 = (bf16[1,16,32,384]{3,2,1,0:T(8,128)(2,1)S(1)}, bf16[1,16,32,384]{3,2,1,0:T(8,128)(2,1)}, u32[]{:S(2)}) copy-start(bf16[1,16,32,384]{3,2,1,0:T(8,128)(2,1)} %param.9) | copy-start | bytes 1179652
  80.7 2.9 %copy-start.1 = (f32[384,192]{1,0:T(8,128)S(1)}, f32[384,192]{1,0:T(8,128)}, u32[]{:S(2)}) copy-start(f32[384,192]{1,0:T(8,128)} %copy-done) | copy-start | bytes 884740
  80.7 5.9 %collective-permute-start.3 = (bf16[1,4,32,384]{3,2,1,0:T(8,128)(2,1)S(1)}, bf16[1,4,32,384]{3,2,1,0:T(8,128)(2,1)S(1)}, u32[]{:S(2)}, u32[]{:S(2)}) collective-permute-start(bf16[1,4,32,384]{3,2,1,0:T(8,128)(2,1)S(1)} %pad_maximum_fusion.3), channel_id=1, source_target_pairs={{28,0},{0,4},{4,8},{8,12},{12,16},{16,20},{20,24},{24,28},{29,1},{... | collective-permute-start | bytes 294920 | tf_op jit(solution)/shard_map/ppermute | solution.py:25
